TPU v7x, 128 devices: a whole 4x4x4 slice. The times are simulated.
128 devices in a mesh: patch: 32 (over y, z, core), level: 4 (over x).
Axes of the slice: x: 4, y: 4, z: 4, core: 2. Of those that a mesh axis runs over, the one named last changes fastest.
Arguments:
- forcing: bfloat16 [4, 256, 2, 128, 128], P('level', 'patch'), may hold values from -24 to 24
- velocity: bfloat16 [4, 256, 2, 128, 128], P('level', 'patch'), may hold values from -18 to 18
- viscosity: float32 [4, 256, 128, 128], P('level', 'patch'), may hold values from 0.3 to 3
- friction: bfloat16 [4, 256, 128, 128], P('level', 'patch'), may hold values from 0.049804688 to 1
- patch_rows: int32 [4, 32], replicated, may hold values from 0 to 8, as said below
Outputs:
- adjoint: float32 [4, 256, 2, 128, 128], P('level', 'patch')
- gradient: bfloat16 [4, 256, 128, 128], P('level', 'patch')
Inputs may be any that keep to these rules, and one draw needn't show every extreme that they name: patch_rows[l, p] is the number of live rows of level l on patch index p: at most 8 // 2**l, patch_rows[0, p] >= 1 and patch_rows[l + 1, p] <= 2 * patch_rows[l, p]; in every draw some patch index holds the most rows on every level.
All inputs are finite; a program needn't handle non-finite values.
Results may differ from a plain program's by a relative error of at most 0.0005.
Values may be sent and summed in bfloat16 or wider, within the bound.
A program may use at most 128 MiB of HBM per device.

v0:
```python
import jax
import jax.numpy as jnp
from jax import lax
from jax.sharding import PartitionSpec as P

relaxation = 0.5


def with_halo(block, sides, width):
    for axis, dim in sides:
        count = lax.axis_size(axis)
        forward = [(i, i + 1) for i in range(count - 1)]
        backward = [(target, source) for source, target in forward]
        low = lax.ppermute(
            lax.slice_in_dim(block, block.shape[dim] - width, None, axis=dim), axis, forward
        )
        high = lax.ppermute(lax.slice_in_dim(block, 0, width, axis=dim), axis, backward)
        block = jnp.concatenate([low, block, high], axis=dim)
    return block


def passed_along(value, axis, steps):
    count = lax.axis_size(axis)
    first, last = (max(0, -steps), min(count, count - steps))
    return lax.ppermute(value, axis, [(source, source + steps) for source in range(first, last)])


def cell_at(grid, row_step, col_step):
    row_total = grid.shape[-2]
    col_total = grid.shape[-1]
    return grid[
        ..., 1 + row_step : row_total - 1 + row_step, 1 + col_step : col_total - 1 + col_step
    ]


def viscosity_faces(visc_loop):
    centre = cell_at(visc_loop, 0, 0)
    east_cell = cell_at(visc_loop, 0, 1)
    west_cell = cell_at(visc_loop, 0, -1)
    north_cell = cell_at(visc_loop, 1, 0)
    south_cell = cell_at(visc_loop, -1, 0)
    return (
        east_cell,
        west_cell,
        north_cell,
        south_cell,
        0.5 * (centre + east_cell),
        0.5 * (centre + west_cell),
        0.5 * (centre + north_cell),
        0.5 * (centre + south_cell),
    )


def diagonal_terms(face_values, friction_cells):
    east_cell, west_cell, north_cell, south_cell, face_east, face_west, face_north, face_south = (
        face_values
    )
    diag_u = 4.0 * (face_east + face_west) + face_north + face_south + friction_cells
    diag_v = 4.0 * (face_north + face_south) + face_east + face_west + friction_cells
    return jnp.stack([diag_u, diag_v], axis=1)


def operator_cells(loop_cells, face_values, friction_cells):
    east_cell, west_cell, north_cell, south_cell, face_east, face_west, face_north, face_south = (
        face_values
    )
    u_loop = loop_cells[:, 0]
    v_loop = loop_cells[:, 1]
    u_centre = cell_at(u_loop, 0, 0)
    u_east = cell_at(u_loop, 0, 1)
    u_west = cell_at(u_loop, 0, -1)
    u_north = cell_at(u_loop, 1, 0)
    u_south = cell_at(u_loop, -1, 0)
    u_northeast = cell_at(u_loop, 1, 1)
    u_northwest = cell_at(u_loop, 1, -1)
    u_southeast = cell_at(u_loop, -1, 1)
    u_southwest = cell_at(u_loop, -1, -1)
    v_centre = cell_at(v_loop, 0, 0)
    v_east = cell_at(v_loop, 0, 1)
    v_west = cell_at(v_loop, 0, -1)
    v_north = cell_at(v_loop, 1, 0)
    v_south = cell_at(v_loop, -1, 0)
    v_northeast = cell_at(v_loop, 1, 1)
    v_northwest = cell_at(v_loop, 1, -1)
    v_southeast = cell_at(v_loop, -1, 1)
    v_southwest = cell_at(v_loop, -1, -1)
    cross_u = (
        east_cell * (0.5 * (v_northeast - v_southeast))
        - west_cell * (0.5 * (v_northwest - v_southwest))
        + 0.5
        * (
            north_cell * (0.5 * (v_northeast - v_northwest))
            - south_cell * (0.5 * (v_southeast - v_southwest))
        )
    )
    cross_v = (
        north_cell * (0.5 * (u_northeast - u_northwest))
        - south_cell * (0.5 * (u_southeast - u_southwest))
        + 0.5
        * (
            east_cell * (0.5 * (u_northeast - u_southeast))
            - west_cell * (0.5 * (u_northwest - u_southwest))
        )
    )
    result_u = (
        -4.0 * (face_east * (u_east - u_centre) - face_west * (u_centre - u_west))
        - (face_north * (u_north - u_centre) - face_south * (u_centre - u_south))
        - cross_u
        + friction_cells * u_centre
    )
    result_v = (
        -4.0 * (face_north * (v_north - v_centre) - face_south * (v_centre - v_south))
        - (face_east * (v_east - v_centre) - face_west * (v_centre - v_west))
        - cross_v
        + friction_cells * v_centre
    )
    return jnp.stack([result_u, result_v], axis=1)


def assemble_loop(cells, edge_table, indices):
    (
        south_index,
        north_index,
        west_index,
        east_index,
        northeast_index,
        southeast_index,
        northwest_index,
        southwest_index,
    ) = indices
    side_cells = cells.shape[-1]
    south_row = edge_table[south_index]
    north_row = edge_table[north_index]
    west_col = edge_table[west_index]
    east_col = edge_table[east_index]
    corner_northeast = edge_table[northeast_index][:, :, 0]
    corner_southeast = edge_table[southeast_index][:, :, side_cells - 1]
    corner_northwest = edge_table[northwest_index][:, :, 0]
    corner_southwest = edge_table[southwest_index][:, :, side_cells - 1]
    middle = jnp.concatenate([west_col[..., None], cells, east_col[..., None]], axis=-1)
    bottom = jnp.concatenate(
        [corner_southwest[..., None], south_row, corner_southeast[..., None]], axis=-1
    )
    top_row = jnp.concatenate(
        [corner_northwest[..., None], north_row, corner_northeast[..., None]], axis=-1
    )
    return jnp.concatenate([bottom[:, :, None], middle, top_row[:, :, None]], axis=2)


def neighbour_slots(own_rows, left_rows, right_rows, columns, slot_count):
    slot_ids = jnp.arange(slot_count, dtype=jnp.int32)
    row_ids = slot_ids // columns
    col_ids = slot_ids % columns
    alive = row_ids < own_rows
    blank = 6 * slot_count
    inside_west = col_ids > 0
    inside_east = col_ids < columns - 1
    has_south = row_ids >= 1
    has_north = row_ids + 1 < own_rows

    def choose(condition, position):
        return jnp.where(condition & alive, position, blank)

    south_index = choose(has_south, slot_count + slot_ids - columns)
    north_index = choose(has_north, slot_ids + columns)
    west_index = jnp.where(
        inside_west,
        choose(alive, 3 * slot_count + slot_ids - 1),
        choose(row_ids < left_rows, 4 * slot_count + row_ids * columns + columns - 1),
    )
    east_index = jnp.where(
        inside_east,
        choose(alive, 2 * slot_count + slot_ids + 1),
        choose(row_ids < right_rows, 5 * slot_count + row_ids * columns),
    )
    northeast_index = jnp.where(
        inside_east,
        choose(has_north, 2 * slot_count + slot_ids + columns + 1),
        choose(row_ids + 1 < right_rows, 5 * slot_count + (row_ids + 1) * columns),
    )
    southeast_index = jnp.where(
        inside_east,
        choose(has_south, 2 * slot_count + slot_ids - columns + 1),
        choose(has_south & (row_ids - 1 < right_rows), 5 * slot_count + (row_ids - 1) * columns),
    )
    northwest_index = jnp.where(
        inside_west,
        choose(has_north, 3 * slot_count + slot_ids + columns - 1),
        choose(row_ids + 1 < left_rows, 4 * slot_count + (row_ids + 1) * columns + columns - 1),
    )
    southwest_index = jnp.where(
        inside_west,
        choose(has_south, 3 * slot_count + slot_ids - columns - 1),
        choose(
            has_south & (row_ids - 1 < left_rows),
            4 * slot_count + (row_ids - 1) * columns + columns - 1,
        ),
    )
    indices = (
        south_index,
        north_index,
        west_index,
        east_index,
        northeast_index,
        southeast_index,
        northwest_index,
        southwest_index,
    )
    return (indices, alive, row_ids, col_ids)


def with_ghosts(cells, indices):
    comps = cells.shape[1]
    side_cells = cells.shape[-1]
    south_edge = cells[:, :, 0, :]
    north_edge = cells[:, :, side_cells - 1, :]
    west_edge = cells[:, :, :, 0]
    east_edge = cells[:, :, :, side_cells - 1]
    edge_stack = jnp.stack([south_edge, north_edge, west_edge, east_edge])
    slot_count = edge_stack.shape[1]
    received = with_halo(edge_stack[None, 2:], (("patch", 0),), 1)
    left_east = received[0, 1]
    right_west = received[2, 0]
    edge_table = jnp.concatenate(
        [
            edge_stack.reshape(4 * slot_count, comps, side_cells),
            left_east,
            right_west,
            jnp.zeros((1, comps, side_cells), cells.dtype),
        ],
        axis=0,
    )
    return assemble_loop(cells, edge_table, indices)


def join_quadrants(south_west, south_east, north_west, north_east):
    bottom = jnp.concatenate([south_west, south_east], axis=-1)
    top_half = jnp.concatenate([north_west, north_east], axis=-1)
    return jnp.concatenate([bottom, top_half], axis=-2)


def parent_total(slot_count, level_count):
    best = 1
    for tier_index in range(1, level_count):
        fine_columns = 2**tier_index
        fine_rows = slot_count // fine_columns
        needed = (fine_rows - 1) // 2 * (fine_columns // 2) + fine_columns // 2
        best = max(best, needed)
    return min(best, slot_count)


def per_device(forcing, velocity, viscosity, friction, patch_rows):
    level_index = lax.axis_index("level")
    patch_index = lax.axis_index("patch")
    level_count = lax.axis_size("level")
    slot_count = forcing.shape[1]
    side_cells = forcing.shape[-1]
    half_side = side_cells // 2
    columns = jnp.left_shift(jnp.int32(1), level_index)
    level_rows = lax.dynamic_index_in_dim(patch_rows, level_index, 0, keepdims=False)
    padded_rows = jnp.concatenate(
        [jnp.zeros((1,), jnp.int32), level_rows, jnp.zeros((1,), jnp.int32)]
    )
    near_rows = lax.dynamic_slice(padded_rows, (patch_index,), (3,))
    indices, alive, row_ids, col_ids = neighbour_slots(
        near_rows[1], near_rows[0], near_rows[2], columns, slot_count
    )
    live_mask = alive.astype(jnp.float32)[:, None, None, None]
    friction_cells = friction[0].astype(jnp.float32)
    finer_level = jnp.minimum(level_index + 1, level_count - 1)
    finer_all = lax.dynamic_index_in_dim(patch_rows, finer_level, 0, keepdims=False)
    finer_rows = lax.dynamic_index_in_dim(finer_all, patch_index, 0, keepdims=False)
    child_ids = []
    covers = []
    for quad_row in range(2):
        for quad_col in range(2):
            fine_row = 2 * row_ids + quad_row
            valid = alive & (fine_row < finer_rows)
            child = jnp.where(valid, fine_row * (2 * columns) + 2 * col_ids + quad_col, slot_count)
            child_ids.append(jnp.minimum(child, slot_count))
            covers.append(
                jnp.broadcast_to(
                    valid.astype(jnp.float32)[:, None, None, None],
                    (slot_count, 1, half_side, half_side),
                )
            )
    covered = join_quadrants(covers[0], covers[1], covers[2], covers[3])
    parent_count = parent_total(slot_count, level_count)
    parent_ids = jnp.minimum(row_ids // 2 * (columns // 2) + col_ids // 2, parent_count - 1)
    quad_row_of = (row_ids % 2)[:, None, None, None]
    quad_col_of = (col_ids % 2)[:, None, None, None]
    force_cells = forcing[0].astype(jnp.float32)
    visc_loop = with_ghosts(viscosity[0][:, None], indices)[:, 0]
    face_values = viscosity_faces(visc_loop)
    diagonal = diagonal_terms(face_values, friction_cells)

    def apply_here(cells):
        return operator_cells(with_ghosts(cells, indices), face_values, friction_cells)

    def smooth(right_side, start, from_zero):
        current = start
        if from_zero:
            current = live_mask * (relaxation * right_side / diagonal)
        else:
            current = live_mask * (
                current + relaxation * (right_side - apply_here(current)) / diagonal
            )
        return current

    zero_cells = jnp.zeros((slot_count, 2, side_cells, side_cells), jnp.float32)
    solution = zero_cells
    right_side = zero_cells
    restricted = jnp.zeros((slot_count, 2, half_side // 2, 2 * half_side), jnp.float32)
    for section in range(level_count - 1, -1, -1):
        active = level_index == section
        if section == level_count - 1:
            candidate = live_mask * force_cells
        else:
            received = passed_along(restricted, "level", -1)
            quads = received.reshape(slot_count, 2, half_side, half_side)
            quad_table = jnp.concatenate(
                [quads, jnp.zeros((1, 2, half_side, half_side), jnp.float32)], axis=0
            )
            placed = join_quadrants(
                quad_table[child_ids[0]],
                quad_table[child_ids[1]],
                quad_table[child_ids[2]],
                quad_table[child_ids[3]],
            )
            candidate = live_mask * ((1.0 - covered) * force_cells + placed)
        right_side = jnp.where(active, candidate, right_side)
        solution = jnp.where(active, smooth(right_side, zero_cells, True), solution)
        if section > 0:
            residual = live_mask * (right_side - apply_here(solution))
            summed = residual.reshape(slot_count, 2, half_side, 2, half_side, 2).sum(axis=(3, 5))
            restricted = summed.reshape(slot_count, 2, half_side // 2, 2 * half_side)
    for section in range(1, level_count):
        parents_here = passed_along(solution[:parent_count], "level", 1)
        parents = parents_here[parent_ids]
        half_rows = jnp.where(
            quad_row_of == 0, parents[:, :, :half_side, :], parents[:, :, half_side:, :]
        )
        quarter = jnp.where(
            quad_col_of == 0, half_rows[..., :half_side], half_rows[..., half_side:]
        )
        correction = jnp.repeat(jnp.repeat(quarter, 2, axis=2), 2, axis=3)
        active = level_index == section
        updated = smooth(right_side, solution + live_mask * correction, False)
        solution = jnp.where(active, updated, solution)
    speed = velocity[0].astype(jnp.float32)
    product = speed[:, 0] * solution[:, 0] + speed[:, 1] * solution[:, 1]
    gradient = (-(friction_cells * product) * live_mask[:, 0]).astype(jnp.bfloat16)
    return (solution[None], gradient[None])


def solution(mesh):
    in_specs = (
        P("level", "patch", None, None, None),
        P("level", "patch", None, None, None),
        P("level", "patch", None, None),
        P("level", "patch", None, None),
        P(),
    )
    out_specs = (P("level", "patch", None, None, None), P("level", "patch", None, None))
    return jax.shard_map(
        per_device, mesh=mesh, in_specs=in_specs, out_specs=out_specs, check_vma=False
    )
```

profile of v0, /device:TPU:30, one launch (start us, length us, event | category | flops | bytes accessed | tf_op | source)
XLA Modules:
  0.0 673.6 jit_solution(11070634638290010228)
XLA Ops:
  1.9 5.6 collective-permute-start.1
  20.7 11.4 %copy.455 = f32[1,8,2,128,128]{1,4,3,2,0:T(8,128)} copy(bf16[1,8,2,128,128]{3,1,4,2,0:T(8,128)(2,1)S(1)} %copy.452) | data formatting | bytes 1572864 | tf_op jit(solution)/shard_map/convert_element_type | solution.py:292
  32.1 21.9 %copy.456 = f32[8,2,64,2,64,2]{4,2,5,3,1,0:T(8,128)} copy(f32[8,2,64,2,64,2]{0,5,4,3,2,1:T(2,128)} %bitcast.412) | data formatting | bytes 2097152 | tf_op jit(solution)/shard_map/convert_element_type | solution.py:292
  62.7 5.8 collective-permute-start.3
  91.8 8.3 %copy.480 = f32[8,128,128]{0,2,1:T(8,128)} copy(f32[8,128,128]{1,0,2:T(8,128)} %fusion.60) | data formatting | bytes 1048576 | tf_op jit(solution)/shard_map/add | solution.py:112
  100.1 11.5 %copy.482 = f32[8,1,64,2,64,2]{4,2,5,3,1,0:T(8,128)} copy(f32[8,1,64,2,64,2]{0,5,4,3,2,1:T(2,128)} %bitcast.431) | data formatting | bytes 1048576 | tf_op jit(solution)/shard_map/stack | solution.py:117
  111.6 8.3 %copy.479 = f32[8,128,128]{0,2,1:T(8,128)} copy(f32[8,128,128]{1,0,2:T(8,128)} %fusion.59) | data formatting | bytes 1048576 | tf_op jit(solution)/shard_map/add | solution.py:106
  119.9 11.5 %copy.481 = f32[8,1,64,2,64,2]{4,2,5,3,1,0:T(8,128)} copy(f32[8,1,64,2,64,2]{0,5,4,3,2,1:T(2,128)} %bitcast.432) | data formatting | bytes 1048576 | tf_op jit(solution)/shard_map/stack | solution.py:117
  147.6 5.9 copy.453
  153.5 11.5 %copy.454 = f32[8,64,2,64,2]{3,1,4,2,0:T(8,128)} copy(f32[8,64,2,64,2]{0,4,3,2,1:T(2,128)} %bitcast.433) | data formatting | bytes 1048576 | tf_op jit(solution)/shard_map/sub | solution.py:330
  190.8 5.3 collective-permute-start.6
  203.2 14.2 %copy.489 = f32[8,2,128,128]{0,3,2,1:T(8,128)} copy(f32[8,2,128,128]{2,0,3,1:T(8,128)} %get-tuple-element.22) | data formatting | bytes 2097152 | tf_op jit(solution)/shard_map/concatenate | solution.py:239
  217.5 21.9 %copy.490 = f32[8,2,64,2,64,2]{4,2,5,3,1,0:T(8,128)} copy(f32[8,2,64,2,64,2]{0,5,4,3,2,1:T(2,128)} %bitcast.413) | data formatting | bytes 2097152 | tf_op jit(solution)/shard_map/concatenate | solution.py:239
  255.7 8.3 %copy.506 = f32[8,128,128]{0,2,1:T(8,128)} copy(f32[8,128,128]{1,0,2:T(8,128)} %fusion.62) | data formatting | bytes 1048576 | tf_op jit(solution)/shard_map/add | solution.py:112
  264.0 11.6 %copy.508 = f32[8,1,64,2,64,2]{4,2,5,3,1,0:T(8,128)} copy(f32[8,1,64,2,64,2]{0,5,4,3,2,1:T(2,128)} %bitcast.434) | data formatting | bytes 1048576 | tf_op jit(solution)/shard_map/stack | solution.py:117
  275.6 8.3 %copy.505 = f32[8,128,128]{0,2,1:T(8,128)} copy(f32[8,128,128]{1,0,2:T(8,128)} %fusion.61) | data formatting | bytes 1048576 | tf_op jit(solution)/shard_map/add | solution.py:106
  283.8 11.6 %copy.507 = f32[8,1,64,2,64,2]{4,2,5,3,1,0:T(8,128)} copy(f32[8,1,64,2,64,2]{0,5,4,3,2,1:T(2,128)} %bitcast.435) | data formatting | bytes 1048576 | tf_op jit(solution)/shard_map/stack | solution.py:117
  351.9 14.2 %copy.515 = f32[8,2,128,128]{0,3,2,1:T(8,128)} copy(f32[8,2,128,128]{2,0,3,1:T(8,128)} %get-tuple-element.20) | data formatting | bytes 2097152 | tf_op jit(solution)/shard_map/concatenate | solution.py:239
  366.1 21.9 %copy.516 = f32[8,2,64,2,64,2]{4,2,5,3,1,0:T(8,128)} copy(f32[8,2,64,2,64,2]{0,5,4,3,2,1:T(2,128)} %bitcast.414) | data formatting | bytes 2097152 | tf_op jit(solution)/shard_map/concatenate | solution.py:239
  404.4 8.3 %copy.531 = f32[8,128,128]{0,2,1:T(8,128)} copy(f32[8,128,128]{1,0,2:T(8,128)} %fusion.64) | data formatting | bytes 1048576 | tf_op jit(solution)/shard_map/add | solution.py:112
  412.6 11.5 %copy.533 = f32[8,1,64,2,64,2]{4,2,5,3,1,0:T(8,128)} copy(f32[8,1,64,2,64,2]{0,5,4,3,2,1:T(2,128)} %bitcast.436) | data formatting | bytes 1048576 | tf_op jit(solution)/shard_map/stack | solution.py:117
  424.1 8.3 %copy.530 = f32[8,128,128]{0,2,1:T(8,128)} copy(f32[8,128,128]{1,0,2:T(8,128)} %fusion.63) | data formatting | bytes 1048576 | tf_op jit(solution)/shard_map/add | solution.py:106
  432.4 11.5 %copy.532 = f32[8,1,64,2,64,2]{4,2,5,3,1,0:T(8,128)} copy(f32[8,1,64,2,64,2]{0,5,4,3,2,1:T(2,128)} %bitcast.437) | data formatting | bytes 1048576 | tf_op jit(solution)/shard_map/stack | solution.py:117
  443.9 5.8 fusion.5
  456.8 5.0 collective-permute-start.10
  497.9 9.9 %collective-permute-done.11 = f32[4,2,128,128]{2,0,3,1:T(4,128)} collective-permute-done((f32[4,2,128,128]{2,0,3,1:T(4,128)}, f32[4,2,128,128]{2,0,3,1:T(4,128)}, u32[]{:S(2)}, u32[]{:S(2)}) %collective-permute-start.11) | collective-permute-done | bytes 524320 | tf_op jit(solution)/shard_map/ppermute | solution.py:25
  520.1 5.8 collective-permute-start.13
  554.8 7.6 %collective-permute-done.14 = f32[4,2,128,128]{2,0,3,1:T(4,128)} collective-permute-done((f32[4,2,128,128]{2,0,3,1:T(4,128)S(1)}, f32[4,2,128,128]{2,0,3,1:T(4,128)}, u32[]{:S(2)}, u32[]{:S(2)}) %collective-permute-start.14) | collective-permute-done | bytes 524320 | tf_op jit(solution)/shard_map/ppermute | solution.py:25
  574.9 5.5 collective-permute-start.16
  609.9 7.6 %collective-permute-done.17 = f32[4,2,128,128]{2,0,3,1:T(4,128)} collective-permute-done((f32[4,2,128,128]{2,0,3,1:T(4,128)S(1)}, f32[4,2,128,128]{2,0,3,1:T(4,128)}, u32[]{:S(2)}, u32[]{:S(2)}) %collective-permute-start.17) | collective-permute-done | bytes 524320 | tf_op jit(solution)/shard_map/ppermute | solution.py:25
  629.9 5.0 collective-permute-start.19
  659.8 7.9 %fusion.38 = f32[1,8,2,128,128]{3,1,4,2,0:T(8,128)} fusion(f32[1,8,1,128,128]{3,1,4,2,0:T(8,128)S(1)} %bitcast.461, f32[1,8,1,128,128]{3,1,4,2,0:T(8,128)S(1)} %bitcast.463, f32[1,8,1,128,128]{3,1,4,2,0:T(8,128)S(1)} %bitcast.458, f32[1,8,1,128,128]{3,1,4,2,0:T(8,128)S(1)} %bitcast.460, f32[1,8,2,128,128]{3,1,4,2,0:T(8,128)S(1)} %bitcast.448, ...), kind=kLoop, calls=%fused_computation.152 | loop fusion | flops 15728640 | bytes 12582948 | tf_op jit(solution)/shard_map/jit(_where)/select_n | solution.py:349
  (555 shorter events, 352.6 us)
Async XLA Ops:
  1.9 52.1 %collective-permute-start.1 = (f32[1,2,8,1,128]{4,2,3,1,0:T(8,128)S(1)}, f32[1,2,8,1,128]{4,2,3,1,0:T(8,128)S(1)}, u32[]{:S(2)}, u32[]{:S(2)}) collective-permute-start(f32[1,2,8,1,128]{4,2,3,1,0:T(8,128)S(1)} %maximum_bitcast_fusion.29), channel_id=1, source_target_pairs={{4,0},{8,4},{12,8},{16,12},{20,16},{24,20},{28,24},{32,28},{36,32}... | collective-permute-start | bytes 24584 | tf_op jit(solution)/shard_map/ppermute | solution.py:17
  7.5 46.5 %collective-permute-start = (f32[1,2,8,1,128]{4,2,3,1,0:T(8,128)S(1)}, f32[1,2,8,1,128]{4,2,3,1,0:T(8,128)S(1)}, u32[]{:S(2)}, u32[]{:S(2)}) collective-permute-start(f32[1,2,8,1,128]{4,2,3,1,0:T(8,128)S(1)} %maximum_bitcast_fusion.29), channel_id=1, source_target_pairs={{0,4},{4,8},{8,12},{12,16},{16,20},{20,24},{24,28},{28,32},{32,36}... | collective-permute-start | bytes 24584 | tf_op jit(solution)/shard_map/ppermute | solution.py:14
  18.7 57.1 %copy-start.72 = (s32[1024]{0:T(1024)}, s32[1024]{0:T(1024)S(1)}, u32[]{:S(2)}) copy-start(s32[1024]{0:T(1024)S(1)} %get-tuple-element.92) | copy-start | bytes 12292
  18.7 36.6 %copy-start.74 = (s32[1024]{0:T(1024)}, s32[1024]{0:T(1024)S(1)}, u32[]{:S(2)}) copy-start(s32[1024]{0:T(1024)S(1)} %get-tuple-element.94) | copy-start | bytes 12292
  18.7 37.6 %copy-start.73 = (s32[1024]{0:T(1024)}, s32[1024]{0:T(1024)S(1)}, u32[]{:S(2)}) copy-start(s32[1024]{0:T(1024)S(1)} %get-tuple-element.95) | copy-start | bytes 12292
  18.7 38.1 %copy-start.76 = (s32[1024]{0:T(1024)}, s32[1024]{0:T(1024)S(1)}, u32[]{:S(2)}) copy-start(s32[1024]{0:T(1024)S(1)} %get-tuple-element.96) | copy-start | bytes 12292
  18.7 38.7 %copy-start.75 = (s32[1024]{0:T(1024)}, s32[1024]{0:T(1024)S(1)}, u32[]{:S(2)}) copy-start(s32[1024]{0:T(1024)S(1)} %get-tuple-element.97) | copy-start | bytes 12292
  20.1 37.9 %copy-start.78 = (s32[1024]{0:T(1024)}, s32[1024]{0:T(1024)S(1)}, u32[]{:S(2)}) copy-start(s32[1024]{0:T(1024)S(1)} %get-tuple-element.98) | copy-start | bytes 12292
  20.1 38.5 %copy-start.77 = (s32[1024]{0:T(1024)}, s32[1024]{0:T(1024)S(1)}, u32[]{:S(2)}) copy-start(s32[1024]{0:T(1024)S(1)} %get-tuple-element.99) | copy-start | bytes 12292
  62.7 12.7 %collective-permute-start.3 = (f32[1,2,8,2,128]{4,2,3,1,0:T(8,128)S(1)}, f32[1,2,8,2,128]{4,2,3,1,0:T(8,128)S(1)}, u32[]{:S(2)}, u32[]{:S(2)}) collective-permute-start(f32[1,2,8,2,128]{4,2,3,1,0:T(8,128)S(1)} %maximum_bitcast_fusion.11), channel_id=1, source_target_pairs={{4,0},{8,4},{12,8},{16,12},{20,16},{24,20},{28,24},{32,28},{36,32}... | collective-permute-start | bytes 49160 | tf_op jit(solution)/shard_map/ppermute | solution.py:17
  68.4 7.2 %collective-permute-start.2 = (f32[1,2,8,2,128]{4,2,3,1,0:T(8,128)S(1)}, f32[1,2,8,2,128]{4,2,3,1,0:T(8,128)S(1)}, u32[]{:S(2)}, u32[]{:S(2)}) collective-permute-start(f32[1,2,8,2,128]{4,2,3,1,0:T(8,128)S(1)} %maximum_bitcast_fusion.11), channel_id=1, source_target_pairs={{0,4},{4,8},{8,12},{12,16},{16,20},{20,24},{24,28},{28,32},{32,36}... | collective-permute-start | bytes 49160 | tf_op jit(solution)/shard_map/ppermute | solution.py:14
  142.1 23.0 %collective-permute-start.4 = (f32[8,2,32,128]{3,2,1,0:T(8,128)}, f32[8,2,32,128]{3,2,1,0:T(8,128)}, u32[]{:S(2)}, u32[]{:S(2)}) collective-permute-start(f32[8,2,32,128]{3,2,1,0:T(8,128)} %copy.484), channel_id=1, source_target_pairs={{1,0},{2,1},{3,2},{5,4},{6,5},{7,6},{9,8},{10,9},{11,10},{13,12},{... | collective-permute-start | bytes 786440 | tf_op jit(solution)/shard_map/ppermute | solution.py:25
  145.6 23.4 %copy-start.82 = (s32[1024]{0:T(1024)}, s32[1024]{0:T(1024)S(1)}, u32[]{:S(2)}) copy-start(s32[1024]{0:T(1024)S(1)} %pad_clamp_fusion.1) | copy-start | bytes 12292
  165.1 17.4 %copy-start.83 = (s32[1024]{0:T(1024)}, s32[1024]{0:T(1024)S(1)}, u32[]{:S(2)}) copy-start(s32[1024]{0:T(1024)S(1)} %pad_clamp_fusion.4) | copy-start | bytes 12292
  190.8 48.6 %collective-permute-start.6 = (f32[1,2,8,2,128]{4,2,3,1,0:T(8,128)S(1)}, f32[1,2,8,2,128]{4,2,3,1,0:T(8,128)S(1)}, u32[]{:S(2)}, u32[]{:S(2)}) collective-permute-start(f32[1,2,8,2,128]{4,2,3,1,0:T(8,128)S(1)} %maximum_bitcast_fusion.14), channel_id=1, source_target_pairs={{4,0},{8,4},{12,8},{16,12},{20,16},{24,20},{28,24},{32,28},{36,32}... | collective-permute-start | bytes 49160 | tf_op jit(solution)/shard_map/ppermute | solution.py:17
  196.1 43.3 %collective-permute-start.5 = (f32[1,2,8,2,128]{4,2,3,1,0:T(8,128)S(1)}, f32[1,2,8,2,128]{4,2,3,1,0:T(8,128)S(1)}, u32[]{:S(2)}, u32[]{:S(2)}) collective-permute-start(f32[1,2,8,2,128]{4,2,3,1,0:T(8,128)S(1)} %maximum_bitcast_fusion.14), channel_id=1, source_target_pairs={{0,4},{4,8},{8,12},{12,16},{16,20},{20,24},{24,28},{28,32},{32,36}... | collective-permute-start | bytes 49160 | tf_op jit(solution)/shard_map/ppermute | solution.py:14
  307.4 5.9 collective-permute-start.7
  340.0 48.0 %collective-permute-start.9 = (f32[1,2,8,2,128]{4,2,3,1,0:T(8,128)S(1)}, f32[1,2,8,2,128]{4,2,3,1,0:T(8,128)S(1)}, u32[]{:S(2)}, u32[]{:S(2)}) collective-permute-start(f32[1,2,8,2,128]{4,2,3,1,0:T(8,128)S(1)} %maximum_bitcast_fusion.17), channel_id=1, source_target_pairs={{4,0},{8,4},{12,8},{16,12},{20,16},{24,20},{28,24},{32,28},{36,32}... | collective-permute-start | bytes 49160 | tf_op jit(solution)/shard_map/ppermute | solution.py:17
  344.9 43.1 %collective-permute-start.8 = (f32[1,2,8,2,128]{4,2,3,1,0:T(8,128)S(1)}, f32[1,2,8,2,128]{4,2,3,1,0:T(8,128)S(1)}, u32[]{:S(2)}, u32[]{:S(2)}) collective-permute-start(f32[1,2,8,2,128]{4,2,3,1,0:T(8,128)S(1)} %maximum_bitcast_fusion.17), channel_id=1, source_target_pairs={{0,4},{4,8},{8,12},{12,16},{16,20},{20,24},{24,28},{28,32},{32,36}... | collective-permute-start | bytes 49160 | tf_op jit(solution)/shard_map/ppermute | solution.py:14
  456.8 8.3 %collective-permute-start.10 = (f32[8,2,32,128]{3,2,1,0:T(8,128)}, f32[8,2,32,128]{3,2,1,0:T(8,128)}, u32[]{:S(2)}, u32[]{:S(2)}) collective-permute-start(f32[8,2,32,128]{3,2,1,0:T(8,128)} %copy.535), channel_id=1, source_target_pairs={{1,0},{2,1},{3,2},{5,4},{6,5},{7,6},{9,8},{10,9},{11,10},{13,12},{... | collective-permute-start | bytes 786440 | tf_op jit(solution)/shard_map/ppermute | solution.py:25
  494.1 18.2 %copy-start.79 = (pred[8]{0:T(512)(128)(4,1)S(1)}, pred[8]{0:T(512)(128)(4,1)}, u32[]{:S(2)}) copy-start(pred[8]{0:T(512)(128)(4,1)} %get-tuple-element.12) | copy-start | bytes 28
  494.2 13.6 %collective-permute-start.11 = (f32[4,2,128,128]{2,0,3,1:T(4,128)}, f32[4,2,128,128]{2,0,3,1:T(4,128)}, u32[]{:S(2)}, u32[]{:S(2)}) collective-permute-start(f32[4,2,128,128]{2,0,3,1:T(4,128)} %slice.1125), channel_id=1, source_target_pairs={{0,1},{1,2},{2,3},{4,5},{5,6},{6,7},{8,9},{9,10},{10,11},{12,13},{... | collective-permute-start | bytes 1572872 | tf_op jit(solution)/shard_map/ppermute | solution.py:25
  497.8 15.9 %copy-start.87 = (pred[8]{0:T(512)(128)(4,1)}, pred[8]{0:T(512)(128)(4,1)S(1)}, u32[]{:S(2)}) copy-start(pred[8]{0:T(512)(128)(4,1)S(1)} %fusion.190) | copy-start | bytes 28
  497.8 15.9 %copy-start.86 = (s32[1024]{0:T(1024)}, s32[1024]{0:T(1024)S(1)}, u32[]{:S(2)}) copy-start(s32[1024]{0:T(1024)S(1)} %pad_clamp_fusion) | copy-start | bytes 12292
  520.1 12.5 %collective-permute-start.13 = (f32[1,2,8,2,128]{4,2,3,1,0:T(8,128)S(1)}, f32[1,2,8,2,128]{4,2,3,1,0:T(8,128)S(1)}, u32[]{:S(2)}, u32[]{:S(2)}) collective-permute-start(f32[1,2,8,2,128]{4,2,3,1,0:T(8,128)S(1)} %maximum_bitcast_fusion.20), channel_id=1, source_target_pairs={{4,0},{8,4},{12,8},{16,12},{20,16},{24,20},{28,24},{32,28},{36,32}... | collective-permute-start | bytes 49160 | tf_op jit(solution)/shard_map/ppermute | solution.py:17
  525.8 7.2 %collective-permute-start.12 = (f32[1,2,8,2,128]{4,2,3,1,0:T(8,128)S(1)}, f32[1,2,8,2,128]{4,2,3,1,0:T(8,128)S(1)}, u32[]{:S(2)}, u32[]{:S(2)}) collective-permute-start(f32[1,2,8,2,128]{4,2,3,1,0:T(8,128)S(1)} %maximum_bitcast_fusion.20), channel_id=1, source_target_pairs={{0,4},{4,8},{8,12},{12,16},{16,20},{20,24},{24,28},{28,32},{32,36}... | collective-permute-start | bytes 49160 | tf_op jit(solution)/shard_map/ppermute | solution.py:14
  549.5 13.0 %collective-permute-start.14 = (f32[4,2,128,128]{2,0,3,1:T(4,128)S(1)}, f32[4,2,128,128]{2,0,3,1:T(4,128)}, u32[]{:S(2)}, u32[]{:S(2)}) collective-permute-start(f32[4,2,128,128]{2,0,3,1:T(4,128)S(1)} %slice.1160), channel_id=1, source_target_pairs={{0,1},{1,2},{2,3},{4,5},{5,6},{6,7},{8,9},{9,10},{10,11},{12,13},{... | collective-permute-start | bytes 1572872 | tf_op jit(solution)/shard_map/ppermute | solution.py:25
  574.9 12.2 %collective-permute-start.16 = (f32[1,2,8,2,128]{4,2,3,1,0:T(8,128)S(1)}, f32[1,2,8,2,128]{4,2,3,1,0:T(8,128)S(1)}, u32[]{:S(2)}, u32[]{:S(2)}) collective-permute-start(f32[1,2,8,2,128]{4,2,3,1,0:T(8,128)S(1)} %maximum_bitcast_fusion.23), channel_id=1, source_target_pairs={{4,0},{8,4},{12,8},{16,12},{20,16},{24,20},{28,24},{32,28},{36,32}... | collective-permute-start | bytes 49160 | tf_op jit(solution)/shard_map/ppermute | solution.py:17
  580.3 7.2 %collective-permute-start.15 = (f32[1,2,8,2,128]{4,2,3,1,0:T(8,128)S(1)}, f32[1,2,8,2,128]{4,2,3,1,0:T(8,128)S(1)}, u32[]{:S(2)}, u32[]{:S(2)}) collective-permute-start(f32[1,2,8,2,128]{4,2,3,1,0:T(8,128)S(1)} %maximum_bitcast_fusion.23), channel_id=1, source_target_pairs={{0,4},{4,8},{8,12},{12,16},{16,20},{20,24},{24,28},{28,32},{32,36}... | collective-permute-start | bytes 49160 | tf_op jit(solution)/shard_map/ppermute | solution.py:14
  604.0 13.4 %collective-permute-start.17 = (f32[4,2,128,128]{2,0,3,1:T(4,128)S(1)}, f32[4,2,128,128]{2,0,3,1:T(4,128)}, u32[]{:S(2)}, u32[]{:S(2)}) collective-permute-start(f32[4,2,128,128]{2,0,3,1:T(4,128)S(1)} %slice.1195), channel_id=1, source_target_pairs={{0,1},{1,2},{2,3},{4,5},{5,6},{6,7},{8,9},{9,10},{10,11},{12,13},{... | collective-permute-start | bytes 1572872 | tf_op jit(solution)/shard_map/ppermute | solution.py:25
  629.9 11.9 %collective-permute-start.19 = (f32[1,2,8,2,128]{4,2,3,1,0:T(8,128)S(1)}, f32[1,2,8,2,128]{4,2,3,1,0:T(8,128)S(1)}, u32[]{:S(2)}, u32[]{:S(2)}) collective-permute-start(f32[1,2,8,2,128]{4,2,3,1,0:T(8,128)S(1)} %maximum_bitcast_fusion.26), channel_id=1, source_target_pairs={{4,0},{8,4},{12,8},{16,12},{20,16},{24,20},{28,24},{32,28},{36,32}... | collective-permute-start | bytes 49160 | tf_op jit(solution)/shard_map/ppermute | solution.py:17
  634.9 7.2 %collective-permute-start.18 = (f32[1,2,8,2,128]{4,2,3,1,0:T(8,128)S(1)}, f32[1,2,8,2,128]{4,2,3,1,0:T(8,128)S(1)}, u32[]{:S(2)}, u32[]{:S(2)}) collective-permute-start(f32[1,2,8,2,128]{4,2,3,1,0:T(8,128)S(1)} %maximum_bitcast_fusion.26), channel_id=1, source_target_pairs={{0,4},{4,8},{8,12},{12,16},{16,20},{20,24},{24,28},{28,32},{32,36}... | collective-permute-start | bytes 49160 | tf_op jit(solution)/shard_map/ppermute | solution.py:14
  (84 other events, 353.8 us)
where the time goes:
time: 687 us; the launch traced here: 674 us
  local copies, waits for them, and re-layouts  470 us (68%)
  other arithmetic  99.9 us (15%)
  starting transfers between devices  67.8 us (10%)
  waiting for transfers between devices  33.1 us (5%)
    concatenate x4, local copies, waits for them, and re-layouts, join_quadrants(): return jnp.concatenate([bottom, top_half], axis=-2)  72.2 us
    another operation x6, local copies, waits for them, and re-layouts, operator_cells(): return jnp.stack([result_u, result_v], axis=1)  69.2 us
    unnamed x213, local copies, waits for them, and re-layouts  47.5 us
    ppermute x7, starting transfers between devices, with_halo(): lax.ppermute(lax.slice_in_dim(block, 0, width, axis=dim), axis, backward)  37.7 us
    convert_element_type x2, local copies, waits for them, and re-layouts, per_device(): force_cells = forcing[0].astype(jnp.float32)  33.3 us
    ppermute x6, waiting for transfers between devices, passed_along(): lax.ppermute(value, axis, [(source, source + steps) for source in range(f...  31.8 us
    add x3, local copies, waits for them, and re-layouts, operator_cells(): -4.0 * (face_east * (u_east - u_centre) - face_west * (u_centre - u_west))  24.8 us
    add x3, local copies, waits for them, and re-layouts, operator_cells(): -4.0  24.8 us
  transfers between devices with their start and end apart: 20, of which 9 were waited for; matrix products, arithmetic and copies ran while one was open for 26% of the time, Pallas kernels for 0%

commit v1 on v0

v1 whole, which is shorter than its diff:
```python
import functools

import jax
import jax.numpy as jnp
from jax import lax
from jax.experimental import pallas as pl
from jax.experimental.pallas import tpu as pltpu
from jax.sharding import PartitionSpec as P

MESH = pl.DeviceIdType.MESH
F32 = jnp.float32
BF16 = jnp.bfloat16
SIDE = 128
SLOTS = 8
PAD = 8
TALL = 3 * (SLOTS * SIDE + 2 * PAD)


def split_dot(x, matrix):
    high = x.astype(BF16)
    low = (x - high.astype(F32)).astype(BF16)
    return jnp.dot(high, matrix, preferred_element_type=F32) + jnp.dot(
        low, matrix, preferred_element_type=F32
    )


def kernel(
    levels,
    patches,
    rows_ref,
    forcing_hbm,
    velocity_hbm,
    viscosity_hbm,
    friction_hbm,
    out_ref,
    grad_ref,
    forcing,
    velocity,
    viscosity,
    friction,
    mu,
    fric,
    mu_e,
    mu_w,
    diag_u,
    diag_v,
    half_u,
    half_v,
    b_u,
    b_v,
    x_u,
    x_v,
    ue,
    uw,
    ve,
    vw,
    y_u,
    y_v,
    init_send,
    init_recv,
    down_send,
    down_recv,
    down_edge_send,
    down_edge_recv,
    up_send,
    up_recv,
    up_edge_send,
    up_edge_recv,
    load_sem,
    send_sem,
    recv_sem,
):
    level = lax.axis_index("level")
    patch = lax.axis_index("patch")
    cols = jnp.where(level == 0, 1, jnp.where(level == 1, 2, jnp.where(level == 2, 4, 8)))
    prows = jnp.where(level == 0, 8, jnp.where(level == 1, 4, jnp.where(level == 2, 2, 1)))
    height = prows * SIDE
    pitch = height + 2 * PAD
    has_west = patch > 0
    has_east = patch < patches - 1
    finer = jnp.minimum(level + 1, levels - 1)
    west = jnp.maximum(patch - 1, 0)
    east = jnp.minimum(patch + 1, patches - 1)
    own_rows = rows_ref[level, patch]
    west_rows = jnp.where(has_west, rows_ref[level, west], 0)
    east_rows = jnp.where(has_east, rows_ref[level, east], 0)
    fine_own = rows_ref[finer, patch]
    fine_west = jnp.where(has_west, rows_ref[finer, west], 0)
    fine_east = jnp.where(has_east, rows_ref[finer, east], 0)

    loads = [
        pltpu.make_async_copy(src, dst, load_sem.at[i])
        for i, (src, dst) in enumerate(
            (
                (viscosity_hbm, viscosity),
                (friction_hbm, friction),
                (forcing_hbm, forcing),
                (velocity_hbm, velocity),
            )
        )
    ]
    for load in loads:
        load.start()

    barrier = pltpu.get_barrier_semaphore()
    count = jnp.int32(0)
    for dl in (-1, 0, 1):
        for dp in (-1, 0, 1):
            if dl == 0 and dp == 0:
                continue
            there = (level + dl >= 0) & (level + dl < levels) & (patch + dp >= 0) & (patch + dp < patches)
            count = count + jnp.where(there, 1, 0)

            @pl.when(there)
            def _(dl=dl, dp=dp):
                pl.semaphore_signal(
                    barrier,
                    inc=1,
                    device_id={"level": level + dl, "patch": patch + dp},
                    device_id_type=MESH,
                )

    def base_of(col, row):
        return pl.multiple_of((col * pitch + PAD + row * SIDE).astype(jnp.int32), 8)

    def alive(row, total):
        return jnp.where(row < total, 1.0, 0.0).astype(F32)

    lane = lax.broadcasted_iota(jnp.int32, (SIDE, SIDE), 1)

    zeros = jnp.zeros((PAD, SIDE), F32)

    def clear(col, carry):
        first = pl.multiple_of(col * pitch, 8)
        last = pl.multiple_of(col * pitch + PAD + height, 8)
        for ref in (mu, x_u, x_v, ue, uw, ve, vw):
            ref[pl.ds(first, PAD), :] = zeros
            ref[pl.ds(last, PAD), :] = zeros
        return carry

    lax.fori_loop(0, cols + 2, clear, 0)

    for load in loads[:3]:
        load.wait()

    def unpack(slot_id, carry):
        col = slot_id // prows
        row = slot_id - col * prows
        base = base_of(col + 1, row)
        slot = row * cols + col
        live = alive(row, own_rows)
        mu[pl.ds(base, SIDE), :] = viscosity[slot] * live
        fric[pl.ds(base, SIDE), :] = friction[slot].astype(F32)
        b_u[pl.ds(base, SIDE), :] = forcing[slot, 0].astype(F32) * live
        b_v[pl.ds(base, SIDE), :] = forcing[slot, 1].astype(F32) * live
        return carry

    lax.fori_loop(0, SLOTS, unpack, 0)

    def pack(row, carry):
        for side in range(2):
            base = base_of(jnp.where(side == 0, 1, cols), row)
            near, far = (0, 1) if side == 0 else (SIDE - 1, SIDE - 2)
            mu_t = jnp.transpose(mu[pl.ds(base, SIDE), :])
            fr_t = jnp.transpose(fric[pl.ds(base, SIDE), :])
            bu_t = jnp.transpose(b_u[pl.ds(base, SIDE), :])
            bv_t = jnp.transpose(b_v[pl.ds(base, SIDE), :])
            parts = [
                mu_t[near : near + 1],
                mu_t[far : far + 1],
                fr_t[near : near + 1],
                bu_t[near : near + 1],
                bv_t[near : near + 1],
                jnp.zeros((3, SIDE), F32),
            ]
            init_send[side, row] = jnp.concatenate(parts, axis=0)
        return carry

    lax.fori_loop(0, prows, pack, 0)

    pl.semaphore_wait(barrier, count)

    def copy_to(src, dst, sem, dl, dp):
        return pltpu.make_async_remote_copy(
            src_ref=src,
            dst_ref=dst,
            send_sem=send_sem.at[sem],
            recv_sem=recv_sem.at[sem],
            device_id={"level": level + dl, "patch": patch + dp},
            device_id_type=MESH,
        )

    init_west = copy_to(init_send.at[0], init_recv.at[0], 0, 0, -1)
    init_east = copy_to(init_send.at[1], init_recv.at[1], 1, 0, 1)

    @pl.when(has_west)
    def _():
        init_west.start()

    @pl.when(has_east)
    def _():
        init_east.start()

    @pl.when(has_east)
    def _():
        init_west.wait_recv()

    @pl.when(jnp.logical_not(has_east))
    def _():
        init_recv[0] = jnp.ones((SLOTS, 8, SIDE), F32)

    @pl.when(has_west)
    def _():
        init_east.wait_recv()

    @pl.when(jnp.logical_not(has_west))
    def _():
        init_recv[1] = jnp.ones((SLOTS, 8, SIDE), F32)

    def spread(tile_t, index, first=0, count=SIDE):
        return jnp.broadcast_to(tile_t[first : first + count, index : index + 1], (count, SIDE))

    def unpack_halo(row, carry):
        for side in range(2):
            col = cols + 1 if side == 0 else 0
            base = base_of(jnp.int32(0) + col, row)
            near = 0 if side == 0 else SIDE - 1
            live = alive(row, east_rows if side == 0 else west_rows)
            tile_t = jnp.transpose(init_recv[side, row])
            mu[pl.ds(base, SIDE), :] = (
                jnp.where(lane == near, spread(tile_t, 0), spread(tile_t, 1)) * live
            )
            fric[pl.ds(base, SIDE), :] = spread(tile_t, 2)
            b_u[pl.ds(base, SIDE), :] = spread(tile_t, 3) * live
            b_v[pl.ds(base, SIDE), :] = spread(tile_t, 4) * live
        return carry

    lax.fori_loop(0, prows, unpack_halo, 0)

    def coefficients(index, carry):
        col = index // prows
        row = index - col * prows
        base = base_of(col, row)
        to_east = pl.multiple_of(base + jnp.where(col == cols + 1, 0, pitch), 8)
        to_west = pl.multiple_of(base - jnp.where(col == 0, 0, pitch), 8)
        total = jnp.where(col == 0, west_rows, jnp.where(col == cols + 1, east_rows, own_rows))
        live = 0.5 * alive(row, total)
        here = mu[pl.ds(base, SIDE), :]
        m_e = pltpu.roll(jnp.where(lane == 0, mu[pl.ds(to_east, SIDE), :], here), SIDE - 1, 1)
        m_w = pltpu.roll(jnp.where(lane == SIDE - 1, mu[pl.ds(to_west, SIDE), :], here), 1, 1)
        across = m_e + m_w + 2.0 * here
        along = mu[pl.ds(base + 1, SIDE), :] + mu[pl.ds(base - 1, SIDE), :] + 2.0 * here
        fr = fric[pl.ds(base, SIDE), :]
        d_u = 2.0 * across + 0.5 * along + fr
        d_v = 2.0 * along + 0.5 * across + fr
        mu_e[pl.ds(base, SIDE), :] = m_e
        mu_w[pl.ds(base, SIDE), :] = m_w
        diag_u[pl.ds(base, SIDE), :] = d_u
        diag_v[pl.ds(base, SIDE), :] = d_v
        half_u[pl.ds(base, SIDE), :] = live / d_u
        half_v[pl.ds(base, SIDE), :] = live / d_v
        return carry

    lax.fori_loop(0, (cols + 2) * prows, coefficients, 0)

    def shift_pass():
        def body(slot_id, carry):
            col = slot_id // prows
            row = slot_id - col * prows
            base = base_of(col + 1, row)
            to_east = pl.multiple_of(base + pitch, 8)
            to_west = pl.multiple_of(base - pitch, 8)
            for src, dst_e, dst_w in ((x_u, ue, uw), (x_v, ve, vw)):
                here = src[pl.ds(base, SIDE), :]
                dst_e[pl.ds(base, SIDE), :] = pltpu.roll(
                    jnp.where(lane == 0, src[pl.ds(to_east, SIDE), :], here), SIDE - 1, 1
                )
                dst_w[pl.ds(base, SIDE), :] = pltpu.roll(
                    jnp.where(lane == SIDE - 1, src[pl.ds(to_west, SIDE), :], here), 1, 1
                )
            return carry

        lax.fori_loop(0, SLOTS, body, 0)

    chunk = 64

    def residual_at(base):
        def at(ref, step=0):
            return ref[pl.ds(base + step, chunk), :]

        m, m_e, m_w, m_n, m_s = at(mu), at(mu_e), at(mu_w), at(mu, 1), at(mu, -1)
        p_e, p_w, p_n, p_s = m + m_e, m + m_w, m + m_n, m + m_s
        ue_n, ue_s, uw_n, uw_s = at(ue, 1), at(ue, -1), at(uw, 1), at(uw, -1)
        ve_n, ve_s, vw_n, vw_s = at(ve, 1), at(ve, -1), at(vw, 1), at(vw, -1)
        u, v = at(x_u), at(x_v)
        cross_u = 0.5 * (m_e * (ve_n - ve_s) - m_w * (vw_n - vw_s)) + 0.25 * (
            m_n * (ve_n - vw_n) - m_s * (ve_s - vw_s)
        )
        cross_v = 0.5 * (m_n * (ue_n - uw_n) - m_s * (ue_s - uw_s)) + 0.25 * (
            m_e * (ue_n - ue_s) - m_w * (uw_n - uw_s)
        )
        near_u = 2.0 * (p_e * at(ue) + p_w * at(uw)) + 0.5 * (p_n * at(x_u, 1) + p_s * at(x_u, -1))
        near_v = 2.0 * (p_n * at(x_v, 1) + p_s * at(x_v, -1)) + 0.5 * (p_e * at(ve) + p_w * at(vw))
        r_u = at(b_u) - (at(diag_u) * u - near_u - cross_u)
        r_v = at(b_v) - (at(diag_v) * v - near_v - cross_v)
        return u, v, r_u, r_v

    def chunk_base(index):
        slot_id = index // (SIDE // chunk)
        part = index - slot_id * (SIDE // chunk)
        col = slot_id // prows
        row = slot_id - col * prows
        return pl.multiple_of(base_of(col + 1, row) + part * chunk, 8), row

    fine_lane = lax.broadcasted_iota(jnp.int32, (SIDE, SIDE), 0)
    joins = [
        jnp.where(fine_lane // 2 + half * (SIDE // 2) == lane, 1.0, 0.0).astype(BF16)
        for half in range(2)
    ]
    spreads = [
        jnp.where(lane // 2 + half * (SIDE // 2) == fine_lane, 1.0, 0.0).astype(BF16)
        for half in range(2)
    ]
    quarter = SIDE // 2

    down_main = copy_to(down_send.at[:, pl.ds(0, 256), :], down_recv, 2, -1, 0)
    down_west = copy_to(down_edge_send.at[0], down_edge_recv.at[0], 3, -1, -1)
    down_east = copy_to(down_edge_send.at[1], down_edge_recv.at[1], 4, -1, 1)
    up_main = copy_to(up_send, up_recv, 5, 1, 0)
    up_west = copy_to(up_edge_send.at[0], up_edge_recv.at[0], 6, 1, -1)
    up_east = copy_to(up_edge_send.at[1], up_edge_recv.at[1], 7, 1, 1)
    half_rows = prows // 2

    @pl.when(level < levels - 1)
    def _():
        down_main.wait_recv()

        def place(block, carry):
            col = block // half_rows
            part = block - col * half_rows
            base = pl.multiple_of((col + 1) * pitch + PAD + part * quarter, 8)
            covered = part < fine_own
            got = pl.multiple_of(block * quarter, 8)
            for comp, ref in enumerate((b_u, b_v)):
                ref[pl.ds(base, quarter), :] = jnp.where(
                    covered,
                    down_recv[comp, pl.ds(got, quarter), :],
                    ref[pl.ds(base, quarter), :],
                )
            return carry

        lax.fori_loop(0, 4, place, 0)

    for side in range(2):
        there = has_east if side == 0 else has_west

        @pl.when((level >= 1) & (level < levels - 1) & there)
        def _(side=side):
            (down_west if side == 0 else down_east).wait_recv()
            col = cols + 1 if side == 0 else 0
            total = fine_east if side == 0 else fine_west
            tile_t = jnp.transpose(down_edge_recv[side])
            for part in range(2):
                base = pl.multiple_of(col * pitch + PAD + part * quarter, 8)
                covered = part < total
                for comp, ref in enumerate((b_u, b_v)):
                    ref[pl.ds(base, quarter), :] = jnp.where(
                        covered,
                        spread(tile_t, comp, part * quarter, quarter),
                        ref[pl.ds(base, quarter), :],
                    )

    def start_pass(index, carry):
        col = index // prows
        row = index - col * prows
        base = base_of(col, row)
        x_u[pl.ds(base, SIDE), :] = half_u[pl.ds(base, SIDE), :] * b_u[pl.ds(base, SIDE), :]
        x_v[pl.ds(base, SIDE), :] = half_v[pl.ds(base, SIDE), :] * b_v[pl.ds(base, SIDE), :]
        return carry

    lax.fori_loop(0, (cols + 2) * prows, start_pass, 0)

    @pl.when(level > 0)
    def _():
        shift_pass()

        def residual_pass(index, carry):
            base, row = chunk_base(index)
            live = alive(row, own_rows)
            u, v, r_u, r_v = residual_at(base)
            y_u[pl.ds(base, chunk), :] = r_u * live
            y_v[pl.ds(base, chunk), :] = r_v * live
            return carry

        lax.fori_loop(0, SLOTS * SIDE // chunk, residual_pass, 0)

        def restrict_pass(block, carry):
            pair = block // prows
            row = block - pair * prows
            for comp, ref in enumerate((y_u, y_v)):
                total = None
                for half in range(2):
                    base = base_of(2 * pair + half + 1, row)
                    rows = (
                        ref[pl.ds(base, quarter, stride=2), :]
                        + ref[pl.ds(base + 1, quarter, stride=2), :]
                    )
                    term = split_dot(rows, joins[half])
                    total = term if total is None else total + term
                down_send[comp, pl.ds(pl.multiple_of(block * quarter, 8), quarter), :] = total
            return carry

        lax.fori_loop(0, 4, restrict_pass, 0)
        down_main.start()

    @pl.when(level > 1)
    def _():
        last = pl.multiple_of((cols // 2 - 1) * prows * quarter, 8)
        for side in range(2):
            base = 0 if side == 0 else last
            near = 0 if side == 0 else SIDE - 1
            parts = []
            for comp in range(2):
                block_t = jnp.transpose(down_send[comp, pl.ds(base, SIDE), :])
                parts.append(block_t[near : near + 1])
            parts.append(jnp.zeros((6, SIDE), F32))
            down_edge_send[side] = jnp.concatenate(parts, axis=0)

        @pl.when(has_west)
        def _():
            down_west.start()

        @pl.when(has_east)
        def _():
            down_east.start()

    @pl.when(level > 0)
    def _():
        up_main.wait_recv()

        def prolong(block, carry):
            pair = block // prows
            row = block - pair * prows
            live = alive(row, own_rows)
            for comp, ref in enumerate((x_u, x_v)):
                coarse = up_recv[comp, pl.ds(pl.multiple_of(block * quarter, 8), quarter), :] * live
                for half in range(2):
                    base = base_of(2 * pair + half + 1, row)
                    wide = split_dot(coarse, spreads[half])
                    for step in range(2):
                        where = pl.ds(base + step, quarter, stride=2)
                        ref[where, :] = ref[where, :] + wide
            return carry

        lax.fori_loop(0, 4, prolong, 0)

        for side in range(2):
            there = has_east if side == 0 else has_west

            @pl.when(there)
            def _(side=side):
                (up_west if side == 0 else up_east).wait_recv()
                col = cols + 1 if side == 0 else 0
                total = east_rows if side == 0 else west_rows
                tile_t = jnp.transpose(up_edge_recv[side])
                for part in range(4):

                    @pl.when(part < prows)
                    def _():
                        base = base_of(jnp.int32(0) + col, part)
                        live = alive(part, total)
                        for comp, ref in enumerate((x_u, x_v)):
                            wide = spread(
                                tile_t, 2 * comp + part // 2, (part % 2) * quarter, quarter
                            )
                            for step in range(2):
                                where = pl.ds(base + step, quarter, stride=2)
                                ref[where, :] = ref[where, :] + wide * live

        shift_pass()

        def smooth_pass(index, carry):
            base, row = chunk_base(index)
            u, v, r_u, r_v = residual_at(base)
            y_u[pl.ds(base, chunk), :] = u + half_u[pl.ds(base, chunk), :] * r_u
            y_v[pl.ds(base, chunk), :] = v + half_v[pl.ds(base, chunk), :] * r_v
            return carry

        lax.fori_loop(0, SLOTS * SIDE // chunk, smooth_pass, 0)

    @pl.when(level == 0)
    def _():
        def keep(row, carry):
            base = base_of(1, row)
            y_u[pl.ds(base, SIDE), :] = x_u[pl.ds(base, SIDE), :]
            y_v[pl.ds(base, SIDE), :] = x_v[pl.ds(base, SIDE), :]
            return carry

        lax.fori_loop(0, SLOTS, keep, 0)

    @pl.when(level < levels - 1)
    def _():
        def collect(block, carry):
            col = block // half_rows
            part = block - col * half_rows
            base = pl.multiple_of((col + 1) * pitch + PAD + part * quarter, 8)
            for comp, ref in enumerate((y_u, y_v)):
                up_send[comp, pl.ds(pl.multiple_of(block * quarter, 8), quarter), :] = ref[
                    pl.ds(base, quarter), :
                ]
            return carry

        lax.fori_loop(0, 4, collect, 0)
        up_main.start()
        for side in range(2):
            col = 1 if side == 0 else cols
            near = 0 if side == 0 else SIDE - 1
            parts = []
            for ref in (y_u, y_v):
                for part in range(2):
                    base = base_of(jnp.int32(0) + col, part)
                    block_t = jnp.transpose(ref[pl.ds(base, SIDE), :])
                    parts.append(block_t[near : near + 1])
            parts.append(jnp.zeros((4, SIDE), F32))
            up_edge_send[side] = jnp.concatenate(parts, axis=0)

        @pl.when(has_west)
        def _():
            up_west.start()

        @pl.when(has_east)
        def _():
            up_east.start()

    loads[3].wait()

    def finish(slot_id, carry):
        col = slot_id // prows
        row = slot_id - col * prows
        base = base_of(col + 1, row)
        slot = row * cols + col
        live = alive(row, own_rows)
        u = y_u[pl.ds(base, SIDE), :]
        v = y_v[pl.ds(base, SIDE), :]
        out_ref[slot, 0] = u
        out_ref[slot, 1] = v
        product = velocity[slot, 0].astype(F32) * u + velocity[slot, 1].astype(F32) * v
        grad_ref[slot] = (-(friction[slot].astype(F32) * product) * live).astype(BF16)
        return carry

    lax.fori_loop(0, SLOTS, finish, 0)

    @pl.when(has_west)
    def _():
        init_west.wait_send()

    @pl.when(has_east)
    def _():
        init_east.wait_send()

    @pl.when(level > 0)
    def _():
        down_main.wait_send()

    @pl.when((level > 1) & has_west)
    def _():
        down_west.wait_send()

    @pl.when((level > 1) & has_east)
    def _():
        down_east.wait_send()

    @pl.when(level < levels - 1)
    def _():
        up_main.wait_send()

    @pl.when((level < levels - 1) & has_west)
    def _():
        up_west.wait_send()

    @pl.when((level < levels - 1) & has_east)
    def _():
        up_east.wait_send()


def per_device(levels, patches, forcing, velocity, viscosity, friction, patch_rows):
    tall = pltpu.VMEM((TALL, SIDE), F32)
    any_space = pl.BlockSpec(memory_space=pl.ANY)
    vmem = pl.BlockSpec(memory_space=pltpu.VMEM)
    adjoint, gradient = pl.pallas_call(
        functools.partial(kernel, levels, patches),
        out_shape=(
            jax.ShapeDtypeStruct((SLOTS, 2, SIDE, SIDE), F32),
            jax.ShapeDtypeStruct((SLOTS, SIDE, SIDE), BF16),
        ),
        in_specs=[pl.BlockSpec(memory_space=pltpu.SMEM)] + [any_space] * 4,
        out_specs=(vmem, vmem),
        scratch_shapes=[
            pltpu.VMEM((SLOTS, 2, SIDE, SIDE), BF16),
            pltpu.VMEM((SLOTS, 2, SIDE, SIDE), BF16),
            pltpu.VMEM((SLOTS, SIDE, SIDE), F32),
            pltpu.VMEM((SLOTS, SIDE, SIDE), BF16),
        ]
        + [tall] * 18
        + [
            pltpu.VMEM((2, SLOTS, 8, SIDE), F32),
            pltpu.VMEM((2, SLOTS, 8, SIDE), F32),
            pltpu.VMEM((2, 384, SIDE), F32),
            pltpu.VMEM((2, 256, SIDE), F32),
            pltpu.VMEM((2, 8, SIDE), F32),
            pltpu.VMEM((2, 8, SIDE), F32),
            pltpu.VMEM((2, 256, SIDE), F32),
            pltpu.VMEM((2, 256, SIDE), F32),
            pltpu.VMEM((2, 8, SIDE), F32),
            pltpu.VMEM((2, 8, SIDE), F32),
            pltpu.SemaphoreType.DMA((4,)),
            pltpu.SemaphoreType.DMA((8,)),
            pltpu.SemaphoreType.DMA((8,)),
        ],
        compiler_params=pltpu.CompilerParams(
            collective_id=0, has_side_effects=True, vmem_limit_bytes=56 << 20
        ),
    )(patch_rows, forcing[0], velocity[0], viscosity[0], friction[0])
    return adjoint[None], gradient[None]


def solution(mesh):
    in_specs = (
        P("level", "patch", None, None, None),
        P("level", "patch", None, None, None),
        P("level", "patch", None, None),
        P("level", "patch", None, None),
        P(),
    )
    out_specs = (P("level", "patch", None, None, None), P("level", "patch", None, None))
    return jax.shard_map(
        functools.partial(per_device, mesh.shape["level"], mesh.shape["patch"]),
        mesh=mesh,
        in_specs=in_specs,
        out_specs=out_specs,
        check_vma=False,
    )
```

time: 687 us -> 87.6 us (0.13); the launches traced: 674 us -> 87.5 us
  local copies, waits for them, and re-layouts: 470 us -> 3.04 us
  other arithmetic: 99.9 us -> 0 us
  Pallas kernels: 0 us -> 83.8 us
  starting transfers between devices: 67.8 us -> 0 us
  waiting for transfers between devices: 33.1 us -> 0 us
    gather x95 -> x0, local copies, waits for them, and re-layouts: 100 us -> none  [the longest x6 13.8 us: per_device(): quad_table[child_ids[1]]]
    pallas_call x0 -> x1, Pallas kernels: none -> 83.8 us  [per_device(): pl.pallas_call(functools.partial(kernel, levels, patches), out_shape=(jax...]
    concatenate x8 -> x0, local copies, waits for them, and re-layouts: 78.1 us -> none  [the longest x4 72.2 us: join_quadrants(): return jnp.concatenate([bottom, top_half], axis=-2)]
    another operation x13 -> x0, local copies, waits for them, and re-layouts: 69.2 us -> none  [the longest x6 69.2 us: operator_cells(): return jnp.stack([result_u, result_v], axis=1)]
    ppermute x20 -> x0, starting transfers between devices: 67.8 us -> none  [the longest x7 37.7 us: with_halo(): lax.ppermute(lax.slice_in_dim(block, 0, width, axis=dim), axis, backward)]
    add x6 -> x0, local copies, waits for them, and re-layouts: 49.6 us -> none  [the longest x3 24.8 us: operator_cells(): -4.0 * (face_east * (u_east - u_centre) - face_west * (u_centre - u_west))]
    unnamed x213 -> x4, local copies, waits for them, and re-layouts: 47.5 us -> 3.04 us
    convert_element_type x2 -> x0, local copies, waits for them, and re-layouts: 33.3 us -> none  [per_device(): force_cells = forcing[0].astype(jnp.float32)]
  transfers between devices with their start and end apart: 20 -> 0, of which waited for: 9 -> 0; matrix products, arithmetic and copies ran while one was open for 26% -> 0% of each run, Pallas kernels for 0% -> 0%
where the time goes in v1:
time: 87.6 us; the launch traced here: 87.5 us
  Pallas kernels  83.8 us (96%)
  local copies, waits for them, and re-layouts  3.04 us (3%)
    pallas_call x1, Pallas kernels, per_device(): pl.pallas_call(functools.partial(kernel, levels, patches), out_shape=(jax...  83.8 us
    unnamed x4, local copies, waits for them, and re-layouts  3.04 us

profile of v1, /device:TPU:30, one launch (start us, length us, event | category | flops | bytes accessed | tf_op | source)
XLA Modules:
  0.0 87.5 jit_solution(5236261884755115120)
XLA Ops:
  0.6 83.8 %shard_map.68 = (f32[8,2,128,128]{3,2,1,0:T(8,128)}, bf16[8,128,128]{2,1,0:T(8,128)(2,1)}) custom-call(s32[4,32]{1,0:T(4,128)} %rows_ref.1, bf16[8,2,128,128]{3,2,1,0:T(8,128)(2,1)} %bitcast.7, bf16[8,2,128,128]{3,2,1,0:T(8,128)(2,1)} %bitcast.8, f32[8,128,128]{2,1,0:T(8,128)} %bitcast.9, bf16[8,128,128]{2,1,0:T(8,128)(2,1)} %bitcast.11), custom_call_target="tpu_custom_call" | custom-call | tf_op jit(solution)/shard_map/pallas_call | solution.py:590
  84.4 0.0 copy-start
  84.4 2.3 %copy.9 = f32[1,8,2,128,128]{4,3,2,1,0:T(8,128)} copy(f32[1,8,2,128,128]{4,3,2,1,0:T(8,128)} %bitcast.6) | data formatting | bytes 2097152
  86.7 0.0 copy-done
  86.7 0.7 copy.10
Async XLA Ops:
  84.4 2.4 %copy-start = (bf16[8,128,128]{2,1,0:T(8,128)(2,1)S(1)}, bf16[8,128,128]{2,1,0:T(8,128)(2,1)}, u32[]{:S(2)}) copy-start(bf16[8,128,128]{2,1,0:T(8,128)(2,1)} %get-tuple-element.5) | copy-start | bytes 786436

commit v2 on v1

v2 whole, which is shorter than its diff:
```python
import functools

import jax
import jax.numpy as jnp
from jax import lax
from jax.experimental import pallas as pl
from jax.experimental.pallas import tpu as pltpu
from jax.sharding import PartitionSpec as P

MESH = pl.DeviceIdType.MESH
F32 = jnp.float32
BF16 = jnp.bfloat16
SIDE = 128
SLOTS = 8
PAD = 8
TALL = 3 * (SLOTS * SIDE + 2 * PAD)


def split_dot(x, matrix):
    high = x.astype(BF16)
    low = (x - high.astype(F32)).astype(BF16)
    return jnp.dot(high, matrix, preferred_element_type=F32) + jnp.dot(
        low, matrix, preferred_element_type=F32
    )


START_ROWS = {
    0: {0: (256, 1024), 1: (72, 256), 2: (24, 72), 3: (0, 24)},
    1: {1: (128, 512), 2: (40, 128), 3: (0, 40)},
    2: {2: (64, 256), 3: (0, 64)},
    3: {3: (0, 128)},
}
RESIDUAL_ROWS = {
    1: {1: (144, 512), 2: (48, 144), 3: (0, 48)},
    2: {2: (80, 256), 3: (0, 80)},
    3: {3: (0, 128)},
}
SMOOTH_ROWS = {
    1: {1: (152, 512), 2: (56, 152), 3: (0, 56)},
    2: {2: (120, 256), 3: (0, 120)},
    3: {3: (0, 128)},
}
SENT_UP = {
    0: {1: (72, 256), 2: (24, 72), 3: (0, 24)},
    1: {2: (56, 128), 3: (0, 56)},
    2: {3: (0, 64)},
}
ORDER = {
    0: (("down", 0), ("down", 1), ("down", 2), ("down", 3)),
    1: (("down", 1), ("down", 2), ("down", 3), ("up", 1), ("up", 2), ("up", 3)),
    2: (("down", 2), ("down", 3), ("up", 2), ("up", 3)),
    3: (("down", 3), ("up", 3)),
}


def over(first_col, col_count, rows, most, body):
    low, high = rows
    pieces = -(-(high - low) // most)
    size = -(-(high - low) // (8 * pieces)) * 8

    def step(index, carry):
        col = index // pieces
        part = index - col * pieces
        start = low if pieces == 1 else jnp.minimum(low + part * size, high - size)
        body(first_col + col, start, size)
        return carry

    lax.fori_loop(0, col_count * pieces, step, 0)


def kernel(
    levels,
    patches,
    rows_ref,
    forcing,
    velocity,
    viscosity,
    friction,
    out_ref,
    grad_ref,
    mu,
    fric,
    mu_e,
    mu_w,
    diag_u,
    diag_v,
    half_u,
    half_v,
    b_u,
    b_v,
    x_u,
    x_v,
    z_u,
    z_v,
    ue,
    uw,
    ve,
    vw,
    y_u,
    y_v,
    init_send,
    init_recv,
    down_send_1,
    down_send_2,
    down_send_3,
    down_recv_0,
    down_recv_1,
    down_recv_2,
    up_recv_1,
    up_recv_2,
    up_recv_3,
    down_edge_send,
    down_edge_recv,
    up_edge_send,
    up_edge_recv,
    init_sem,
    down_sem,
    down_edge_sem,
    up_sem,
    up_edge_sem,
):
    down_send = {1: down_send_1, 2: down_send_2, 3: down_send_3}
    down_recv = {0: down_recv_0, 1: down_recv_1, 2: down_recv_2}
    up_recv = {1: up_recv_1, 2: up_recv_2, 3: up_recv_3}
    level = lax.axis_index("level")
    patch = lax.axis_index("patch")
    cols = jnp.where(level == 0, 1, jnp.where(level == 1, 2, jnp.where(level == 2, 4, 8)))
    prows = jnp.where(level == 0, 8, jnp.where(level == 1, 4, jnp.where(level == 2, 2, 1)))
    height = prows * SIDE
    pitch = height + 2 * PAD
    has_west = patch > 0
    has_east = patch < patches - 1
    finer = jnp.minimum(level + 1, levels - 1)
    west = jnp.maximum(patch - 1, 0)
    east = jnp.minimum(patch + 1, patches - 1)
    own_rows = rows_ref[level, patch]
    west_rows = jnp.where(has_west, rows_ref[level, west], 0)
    east_rows = jnp.where(has_east, rows_ref[level, east], 0)
    fine_own = rows_ref[finer, patch]
    fine_west = jnp.where(has_west, rows_ref[finer, west], 0)
    fine_east = jnp.where(has_east, rows_ref[finer, east], 0)

    barrier = pltpu.get_barrier_semaphore()
    count = jnp.int32(0)
    for dl in (-1, 0, 1):
        for dp in (-1, 0, 1):
            if dl == 0 and dp == 0:
                continue
            there = (level + dl >= 0) & (level + dl < levels) & (patch + dp >= 0) & (patch + dp < patches)
            count = count + jnp.where(there, 1, 0)

            @pl.when(there)
            def _(dl=dl, dp=dp):
                pl.semaphore_signal(
                    barrier,
                    inc=1,
                    device_id={"level": level + dl, "patch": patch + dp},
                    device_id_type=MESH,
                )

    def base_of(col, row):
        return pl.multiple_of((col * pitch + PAD + row * SIDE).astype(jnp.int32), 8)

    def alive(row, total):
        return jnp.where(row < total, 1.0, 0.0).astype(F32)

    lane = lax.broadcasted_iota(jnp.int32, (SIDE, SIDE), 1)

    zeros = jnp.zeros((PAD, SIDE), F32)

    def clear(col, carry):
        first = pl.multiple_of(col * pitch, 8)
        last = pl.multiple_of(col * pitch + PAD + height, 8)
        for ref in (mu, x_u, x_v, z_u, z_v, ue, uw, ve, vw):
            ref[pl.ds(first, PAD), :] = zeros
            ref[pl.ds(last, PAD), :] = zeros
        return carry

    lax.fori_loop(0, cols + 2, clear, 0)

    def unpack(slot_id, carry):
        col = slot_id // prows
        row = slot_id - col * prows
        base = base_of(col + 1, row)
        slot = row * cols + col
        live = alive(row, own_rows)
        mu[pl.ds(base, SIDE), :] = viscosity[slot] * live
        fric[pl.ds(base, SIDE), :] = friction[slot].astype(F32)
        b_u[pl.ds(base, SIDE), :] = forcing[slot, 0].astype(F32) * live
        b_v[pl.ds(base, SIDE), :] = forcing[slot, 1].astype(F32) * live
        return carry

    lax.fori_loop(0, SLOTS, unpack, 0)

    def pack(row, carry):
        for side in range(2):
            base = base_of(jnp.where(side == 0, 1, cols), row)
            near, far = (0, 1) if side == 0 else (SIDE - 1, SIDE - 2)
            mu_t = jnp.transpose(mu[pl.ds(base, SIDE), :])
            fr_t = jnp.transpose(fric[pl.ds(base, SIDE), :])
            bu_t = jnp.transpose(b_u[pl.ds(base, SIDE), :])
            bv_t = jnp.transpose(b_v[pl.ds(base, SIDE), :])
            parts = [
                mu_t[near : near + 1],
                mu_t[far : far + 1],
                fr_t[near : near + 1],
                bu_t[near : near + 1],
                bv_t[near : near + 1],
                jnp.zeros((3, SIDE), F32),
            ]
            init_send[side, row] = jnp.concatenate(parts, axis=0)
        return carry

    lax.fori_loop(0, prows, pack, 0)

    pl.semaphore_wait(barrier, count)

    def copy_to(src, dst, send, recv, there, dp):
        return pltpu.make_async_remote_copy(
            src_ref=src,
            dst_ref=dst,
            send_sem=send,
            recv_sem=recv,
            device_id={"level": there, "patch": patch + dp},
            device_id_type=MESH,
        )

    init_west = copy_to(
        init_send.at[0], init_recv.at[0], init_sem.at[0], init_sem.at[2], level, -1
    )
    init_east = copy_to(
        init_send.at[1], init_recv.at[1], init_sem.at[1], init_sem.at[3], level, 1
    )

    @pl.when(has_west)
    def _():
        init_west.start()

    @pl.when(has_east)
    def _():
        init_east.start()

    @pl.when(has_east)
    def _():
        init_west.wait_recv()

    @pl.when(jnp.logical_not(has_east))
    def _():
        init_recv[0] = jnp.ones((SLOTS, 8, SIDE), F32)

    @pl.when(has_west)
    def _():
        init_east.wait_recv()

    @pl.when(jnp.logical_not(has_west))
    def _():
        init_recv[1] = jnp.ones((SLOTS, 8, SIDE), F32)

    def spread(tile_t, index, first=0, count=SIDE):
        return jnp.broadcast_to(tile_t[first : first + count, index : index + 1], (count, SIDE))

    def unpack_halo(row, carry):
        for side in range(2):
            col = cols + 1 if side == 0 else 0
            base = base_of(jnp.int32(0) + col, row)
            near = 0 if side == 0 else SIDE - 1
            live = alive(row, east_rows if side == 0 else west_rows)
            tile_t = jnp.transpose(init_recv[side, row])
            mu[pl.ds(base, SIDE), :] = (
                jnp.where(lane == near, spread(tile_t, 0), spread(tile_t, 1)) * live
            )
            fric[pl.ds(base, SIDE), :] = spread(tile_t, 2)
            b_u[pl.ds(base, SIDE), :] = spread(tile_t, 3) * live
            b_v[pl.ds(base, SIDE), :] = spread(tile_t, 4) * live
        return carry

    lax.fori_loop(0, prows, unpack_halo, 0)

    def coefficients(index, carry):
        col = index // prows
        row = index - col * prows
        base = base_of(col, row)
        to_east = pl.multiple_of(base + jnp.where(col == cols + 1, 0, pitch), 8)
        to_west = pl.multiple_of(base - jnp.where(col == 0, 0, pitch), 8)
        total = jnp.where(col == 0, west_rows, jnp.where(col == cols + 1, east_rows, own_rows))
        live = 0.5 * alive(row, total)
        here = mu[pl.ds(base, SIDE), :]
        m_e = pltpu.roll(jnp.where(lane == 0, mu[pl.ds(to_east, SIDE), :], here), SIDE - 1, 1)
        m_w = pltpu.roll(jnp.where(lane == SIDE - 1, mu[pl.ds(to_west, SIDE), :], here), 1, 1)
        across = m_e + m_w + 2.0 * here
        along = mu[pl.ds(base + 1, SIDE), :] + mu[pl.ds(base - 1, SIDE), :] + 2.0 * here
        fr = fric[pl.ds(base, SIDE), :]
        d_u = 2.0 * across + 0.5 * along + fr
        d_v = 2.0 * along + 0.5 * across + fr
        mu_e[pl.ds(base, SIDE), :] = m_e
        mu_w[pl.ds(base, SIDE), :] = m_w
        diag_u[pl.ds(base, SIDE), :] = d_u
        diag_v[pl.ds(base, SIDE), :] = d_v
        half_u[pl.ds(base, SIDE), :] = live / d_u
        half_v[pl.ds(base, SIDE), :] = live / d_v
        return carry

    first = jnp.where(level == 0, prows, 0)
    last = jnp.where(level == 0, 2 * prows, (cols + 2) * prows)
    lax.fori_loop(first, last, coefficients, 0)

    quarter = SIDE // 2
    lane_row = lax.broadcasted_iota(jnp.int32, (SIDE, SIDE), 0)
    joins = [
        jnp.where(lane_row // 2 + half * quarter == lane, 1.0, 0.0).astype(BF16)
        for half in range(2)
    ]
    spreads = [
        jnp.where(lane // 2 + half * quarter == lane_row, 1.0, 0.0).astype(BF16)
        for half in range(2)
    ]

    def program(lv):
        columns = 2**lv
        tall = SLOTS // columns * SIDE
        step_col = tall + 2 * PAD
        pending = []

        def at_row(col, row):
            return pl.multiple_of(col * step_col + PAD + row, 8)

        def below(start, size, limit):
            rows = lax.broadcasted_iota(jnp.int32, (size, SIDE), 0) + start
            return rows < limit

        def shift(src_u, src_v, rows):
            def body(col, start, size):
                base = at_row(col, start)
                to_east = pl.multiple_of(base + step_col, 8)
                to_west = pl.multiple_of(base - step_col, 8)
                here_lane = lane[:size]
                for src, dst_e, dst_w in ((src_u, ue, uw), (src_v, ve, vw)):
                    here = src[pl.ds(base, size), :]
                    dst_e[pl.ds(base, size), :] = pltpu.roll(
                        jnp.where(here_lane == 0, src[pl.ds(to_east, size), :], here), SIDE - 1, 1
                    )
                    dst_w[pl.ds(base, size), :] = pltpu.roll(
                        jnp.where(here_lane == SIDE - 1, src[pl.ds(to_west, size), :], here), 1, 1
                    )

            over(1, columns, rows, SIDE, body)

        def residual_at(src_u, src_v, base, size):
            def at(ref, step=0):
                return ref[pl.ds(base + step, size), :]

            m, m_e, m_w, m_n, m_s = at(mu), at(mu_e), at(mu_w), at(mu, 1), at(mu, -1)
            p_e, p_w, p_n, p_s = m + m_e, m + m_w, m + m_n, m + m_s
            ue_n, ue_s, uw_n, uw_s = at(ue, 1), at(ue, -1), at(uw, 1), at(uw, -1)
            ve_n, ve_s, vw_n, vw_s = at(ve, 1), at(ve, -1), at(vw, 1), at(vw, -1)
            u, v = at(src_u), at(src_v)
            cross_u = 0.5 * (m_e * (ve_n - ve_s) - m_w * (vw_n - vw_s)) + 0.25 * (
                m_n * (ve_n - vw_n) - m_s * (ve_s - vw_s)
            )
            cross_v = 0.5 * (m_n * (ue_n - uw_n) - m_s * (ue_s - uw_s)) + 0.25 * (
                m_e * (ue_n - ue_s) - m_w * (uw_n - uw_s)
            )
            near_u = 2.0 * (p_e * at(ue) + p_w * at(uw)) + 0.5 * (
                p_n * at(src_u, 1) + p_s * at(src_u, -1)
            )
            near_v = 2.0 * (p_n * at(src_v, 1) + p_s * at(src_v, -1)) + 0.5 * (
                p_e * at(ve) + p_w * at(vw)
            )
            r_u = at(b_u) - (at(diag_u) * u - near_u - cross_u)
            r_v = at(b_v) - (at(diag_v) * v - near_v - cross_v)
            return u, v, r_u, r_v

        def sides():
            return ((0, has_west, has_east, -1), (1, has_east, has_west, 1))

        def down_copies(sender, tier):
            low, high = RESIDUAL_ROWS[sender][tier]
            low, high = low // 2, high // 2
            copies = []
            for k in range(2**sender // 2):
                part = (slice(None), k, pl.ds(low, high - low))
                copies.append(
                    copy_to(
                        down_send[sender].at[part],
                        down_recv[sender - 1].at[part],
                        down_sem.at[0, tier * 4 + k],
                        down_sem.at[1, tier * 4 + k],
                        sender - 1,
                        0,
                    )
                )
            return copies

        def down_edge(sender, tier, side, dp):
            return copy_to(
                down_edge_send.at[tier, side],
                down_edge_recv.at[tier, side],
                down_edge_sem.at[0, tier * 2 + side],
                down_edge_sem.at[1, tier * 2 + side],
                sender - 1,
                dp,
            )

        def up_copies(sender, tier):
            low, high = SENT_UP[sender][tier]
            sources = (x_u, x_v) if sender == 0 else (y_u, y_v)
            pitch_here = SLOTS // 2**sender * SIDE + 2 * PAD
            copies = []
            for k in range(2**sender):
                for comp in range(2):
                    index = tier * 8 + k * 2 + comp
                    copies.append(
                        copy_to(
                            sources[comp].at[pl.ds((k + 1) * pitch_here + PAD + low, high - low)],
                            up_recv[sender + 1].at[comp, k, pl.ds(low, high - low)],
                            up_sem.at[0, index],
                            up_sem.at[1, index],
                            sender + 1,
                            0,
                        )
                    )
            return copies

        def up_edge(sender, tier, side, dp):
            return copy_to(
                up_edge_send.at[tier, side],
                up_edge_recv.at[tier, side],
                up_edge_sem.at[0, tier * 2 + side],
                up_edge_sem.at[1, tier * 2 + side],
                sender + 1,
                dp,
            )

        def start_edges(make, sender, tier):
            for side, there, _, dp in sides():
                copy = make(sender, tier, side, dp)

                @pl.when(there)
                def _(copy=copy):
                    copy.start()

                pending.append((copy, there))

        def wait_edges(make, sender, tier):
            for side, _, there, dp in sides():
                copy = make(sender, tier, side, dp)

                @pl.when(there)
                def _(copy=copy):
                    copy.wait_recv()

        def send_up(tier):
            low, high = SENT_UP[lv][tier]
            sources = (x_u, x_v) if lv == 0 else (y_u, y_v)
            for side in range(2):
                col = 1 if side == 0 else columns
                near = 0 if side == 0 else SIDE - 1
                parts = []
                for ref in sources:
                    for part in range(2):
                        if part * SIDE < high and low < (part + 1) * SIDE:
                            block_t = jnp.transpose(ref[pl.ds(at_row(col, part * SIDE), SIDE), :])
                            parts.append(block_t[near : near + 1])
                        else:
                            parts.append(jnp.zeros((1, SIDE), F32))
                parts.append(jnp.zeros((4, SIDE), F32))
                up_edge_send[tier, side] = jnp.concatenate(parts, axis=0)
            start_edges(up_edge, lv, tier)
            for copy in up_copies(lv, tier):
                copy.start()
                pending.append((copy, None))

        def down(tier):
            rows = START_ROWS[lv][tier]
            low, high = rows
            if tier == lv:

                def start_body(col, start, size):
                    where = pl.ds(at_row(col, start), size)
                    x_u[where, :] = half_u[where, :] * b_u[where, :]
                    x_v[where, :] = half_v[where, :] * b_v[where, :]

                if lv == 0:
                    over(1, 1, rows, SIDE, start_body)
                else:
                    over(0, columns + 2, rows, SIDE, start_body)
            else:
                if lv > 0:
                    wait_edges(down_edge, lv + 1, tier)
                    for side in range(2):
                        col = columns + 1 if side == 0 else 0
                        limit = quarter * (fine_east if side == 0 else fine_west)
                        tile_t = jnp.transpose(down_edge_recv[tier, side])
                        where = pl.ds(at_row(col, low), high - low)
                        keep = below(low, high - low, limit)
                        for comp, (ref, half, to) in enumerate(
                            ((b_u, half_u, x_u), (b_v, half_v, x_v))
                        ):
                            got = spread(tile_t, comp, low, high - low)
                            to[where, :] = half[where, :] * jnp.where(keep, got, ref[where, :])
                for copy in down_copies(lv + 1, tier):
                    copy.wait_recv()

                def place_body(col, start, size):
                    where = pl.ds(at_row(col, start), size)
                    keep = below(start, size, quarter * fine_own)
                    for comp, (ref, half, to) in enumerate(
                        ((b_u, half_u, x_u), (b_v, half_v, x_v))
                    ):
                        got = down_recv[lv][comp, col - 1, pl.ds(start, size), :]
                        new = jnp.where(keep, got, ref[where, :])
                        ref[where, :] = new
                        to[where, :] = half[where, :] * new

                over(1, columns, rows, SIDE, place_body)
            if lv == 0:
                if tier > 0:
                    send_up(tier)
                return
            shift(x_u, x_v, rows)

            def residual_body(col, start, size):
                base = at_row(col, start)
                _, _, r_u, r_v = residual_at(x_u, x_v, base, size)
                y_u[pl.ds(base, size), :] = r_u
                y_v[pl.ds(base, size), :] = r_v

            over(1, columns, RESIDUAL_ROWS[lv][tier], 64, residual_body)
            low, high = RESIDUAL_ROWS[lv][tier]
            low, high = low // 2, high // 2
            pairs = columns // 2
            copies = down_copies(lv, tier)

            def join_pair(k):
                def join_body(_, start, size):
                    for comp, ref in enumerate((y_u, y_v)):
                        total = None
                        for half in range(2):
                            base = at_row(2 * k + half + 1, 2 * start)
                            lines = (
                                ref[pl.ds(base, size, stride=2), :]
                                + ref[pl.ds(base + 1, size, stride=2), :]
                            )
                            term = split_dot(lines, joins[half])
                            total = term if total is None else total + term
                        down_send[lv][comp, k, pl.ds(start, size), :] = total

                over(0, 1, (low, high), 64, join_body)
                copies[k].start()
                pending.append((copies[k], None))

            for k in sorted({0, pairs - 1}):
                join_pair(k)
            if lv > 1:
                for side in range(2):
                    k = 0 if side == 0 else pairs - 1
                    near = 0 if side == 0 else SIDE - 1
                    lines = min(SIDE, tall // 2)
                    parts = []
                    for comp in range(2):
                        block_t = jnp.transpose(down_send[lv][comp, k, pl.ds(0, lines), :])
                        line = block_t[near : near + 1]
                        if lines < SIDE:
                            line = jnp.concatenate([line, line], axis=1)
                        parts.append(line)
                    parts.append(jnp.zeros((6, SIDE), F32))
                    down_edge_send[tier, side] = jnp.concatenate(parts, axis=0)
                start_edges(down_edge, lv, tier)
            for k in range(1, pairs - 1):
                join_pair(k)

        def up(tier):
            low, high = SENT_UP[lv - 1][tier]
            wait_edges(up_edge, lv - 1, tier)
            for side in range(2):
                col = columns + 1 if side == 0 else 0
                limit = quarter * (east_rows if side == 0 else west_rows)
                tile_t = jnp.transpose(up_edge_recv[tier, side])
                for part in range(2):
                    first, last = max(low, part * SIDE), min(high, (part + 1) * SIDE)
                    if first >= last:
                        continue
                    size = last - first
                    keep = below(first, size, limit)
                    for comp, (ref, to) in enumerate(((x_u, z_u), (x_v, z_v))):
                        wide = spread(tile_t, 2 * comp + part, first - part * SIDE, size)
                        wide = jnp.where(keep, wide, 0.0)
                        for step in range(2):
                            where = pl.ds(at_row(col, 2 * first) + step, size, stride=2)
                            to[where, :] = ref[where, :] + wide
            for copy in up_copies(lv - 1, tier):
                copy.wait_recv()

            def prolong_body(k, start, size):
                keep = below(start, size, quarter * own_rows)
                for comp, (ref, to) in enumerate(((x_u, z_u), (x_v, z_v))):
                    coarse = up_recv[lv][comp, k, pl.ds(start, size), :]
                    coarse = jnp.where(keep, coarse, 0.0)
                    for half in range(2):
                        base = at_row(2 * k + half + 1, 2 * start)
                        wide = split_dot(coarse, spreads[half])
                        for step in range(2):
                            where = pl.ds(base + step, size, stride=2)
                            to[where, :] = ref[where, :] + wide

            over(0, columns // 2, (low, high), 64, prolong_body)
            shift(z_u, z_v, (2 * low, 2 * high))

            def smooth_body(col, start, size):
                base = at_row(col, start)
                where = pl.ds(base, size)
                u, v, r_u, r_v = residual_at(z_u, z_v, base, size)
                y_u[where, :] = u + half_u[where, :] * r_u
                y_v[where, :] = v + half_v[where, :] * r_v

            over(1, columns, SMOOTH_ROWS[lv][tier], 64, smooth_body)
            if lv < levels - 1 and tier > lv:
                send_up(tier)

        for stage, tier in ORDER[lv]:
            (down if stage == "down" else up)(tier)

        finals = (x_u, x_v) if lv == 0 else (y_u, y_v)

        def finish(col, start, size):
            base = at_row(col, start)
            row = start // SIDE
            slot = row * columns + col - 1
            live = alive(row, own_rows)
            u = finals[0][pl.ds(base, size), :]
            v = finals[1][pl.ds(base, size), :]
            out_ref[slot, 0] = u
            out_ref[slot, 1] = v
            product = velocity[slot, 0].astype(F32) * u + velocity[slot, 1].astype(F32) * v
            grad_ref[slot] = (-(friction[slot].astype(F32) * product) * live).astype(BF16)

        over(1, columns, (0, tall), SIDE, finish)
        for copy, there in pending:
            if there is None:
                copy.wait_send()
            else:

                @pl.when(there)
                def _(copy=copy):
                    copy.wait_send()

    for lv in range(levels):

        @pl.when(level == lv)
        def _(lv=lv):
            program(lv)

    @pl.when(has_west)
    def _():
        init_west.wait_send()

    @pl.when(has_east)
    def _():
        init_east.wait_send()


def per_device(levels, patches, forcing, velocity, viscosity, friction, patch_rows):
    tall = pltpu.VMEM((TALL, SIDE), F32)
    vmem = pl.BlockSpec(memory_space=pltpu.VMEM)
    coarse = {
        sender: pltpu.VMEM((2, 2**sender // 2, SLOTS // 2**sender * SIDE // 2, SIDE), F32)
        for sender in range(1, levels)
    }
    adjoint, gradient = pl.pallas_call(
        functools.partial(kernel, levels, patches),
        out_shape=(
            jax.ShapeDtypeStruct((SLOTS, 2, SIDE, SIDE), F32),
            jax.ShapeDtypeStruct((SLOTS, SIDE, SIDE), BF16),
        ),
        in_specs=[pl.BlockSpec(memory_space=pltpu.SMEM)] + [vmem] * 4,
        out_specs=(vmem, vmem),
        scratch_shapes=[tall] * 20
        + [
            pltpu.VMEM((2, SLOTS, 8, SIDE), F32),
            pltpu.VMEM((2, SLOTS, 8, SIDE), F32),
        ]
        + [coarse[sender] for sender in range(1, levels)] * 3
        + [pltpu.VMEM((4, 2, 8, SIDE), F32)] * 4
        + [
            pltpu.SemaphoreType.DMA((4,)),
            pltpu.SemaphoreType.DMA((2, 16)),
            pltpu.SemaphoreType.DMA((2, 8)),
            pltpu.SemaphoreType.DMA((2, 32)),
            pltpu.SemaphoreType.DMA((2, 8)),
        ],
        compiler_params=pltpu.CompilerParams(
            collective_id=0, has_side_effects=True, vmem_limit_bytes=44 << 20
        ),
    )(patch_rows, forcing[0], velocity[0], viscosity[0], friction[0])
    return adjoint[None], gradient[None]


def solution(mesh):
    in_specs = (
        P("level", "patch", None, None, None),
        P("level", "patch", None, None, None),
        P("level", "patch", None, None),
        P("level", "patch", None, None),
        P(),
    )
    out_specs = (P("level", "patch", None, None, None), P("level", "patch", None, None))
    return jax.shard_map(
        functools.partial(per_device, mesh.shape["level"], mesh.shape["patch"]),
        mesh=mesh,
        in_specs=in_specs,
        out_specs=out_specs,
        check_vma=False,
    )
```

time: 87.6 us -> 58.5 us (0.67)
  Pallas kernels: 83.8 us -> 51.1 us
  local copies, waits for them, and re-layouts: 3.04 us -> 6.42 us
    pallas_call x1, Pallas kernels: 83.8 us -> 51.1 us  [per_device(): pl.pallas_call(functools.partial(kernel, levels, patches), out_shape=(jax...]
    unnamed x4 -> x12, local copies, waits for them, and re-layouts: 3.04 us -> 6.42 us
where the time goes in v2:
time: 58.5 us; the launch traced here: 58.2 us
  Pallas kernels  51.1 us (87%)
  local copies, waits for them, and re-layouts  6.42 us (11%)
  between operations  0.65 us (1%)
    pallas_call x1, Pallas kernels, per_device(): pl.pallas_call(functools.partial(kernel, levels, patches), out_shape=(jax...  51.1 us
    unnamed x12, local copies, waits for them, and re-layouts  6.42 us

profile of v2, /device:TPU:30, one launch (start us, length us, event | category | flops | bytes accessed | tf_op | source)
XLA Modules:
  0.0 58.2 jit_solution(9746047673236624733)
XLA Ops:
  0.6 0.0 copy-start.4
  0.6 0.7 %copy-done.4 = s32[4,32]{1,0:T(4,128)S(1)} copy-done((s32[4,32]{1,0:T(4,128)S(1)}, s32[4,32]{1,0:T(4,128)}, u32[]{:S(2)}) %copy-start.4) | copy-done | bytes 536
  1.3 0.0 copy-start
  1.3 1.0 %copy-done = bf16[1,8,2,128,128]{4,3,2,1,0:T(8,128)(2,1)S(1)} copy-done((bf16[1,8,2,128,128]{4,3,2,1,0:T(8,128)(2,1)S(1)}, bf16[1,8,2,128,128]{4,3,2,1,0:T(8,128)(2,1)}, u32[]{:S(2)}) %copy-start) | copy-done | bytes 524312
  2.4 0.0 copy-start.1
  2.4 1.0 %copy-done.1 = bf16[1,8,2,128,128]{4,3,2,1,0:T(8,128)(2,1)S(1)} copy-done((bf16[1,8,2,128,128]{4,3,2,1,0:T(8,128)(2,1)S(1)}, bf16[1,8,2,128,128]{4,3,2,1,0:T(8,128)(2,1)}, u32[]{:S(2)}) %copy-start.1) | copy-done | bytes 524312
  3.4 0.0 copy-start.2
  3.4 1.0 %copy-done.2 = f32[1,8,128,128]{3,2,1,0:T(8,128)S(1)} copy-done((f32[1,8,128,128]{3,2,1,0:T(8,128)S(1)}, f32[1,8,128,128]{3,2,1,0:T(8,128)}, u32[]{:S(2)}) %copy-start.2) | copy-done | bytes 524312
  4.4 0.0 copy-start.3
  4.4 0.9 %copy-done.3 = bf16[1,8,128,128]{3,2,1,0:T(8,128)(2,1)S(1)} copy-done((bf16[1,8,128,128]{3,2,1,0:T(8,128)(2,1)S(1)}, bf16[1,8,128,128]{3,2,1,0:T(8,128)(2,1)}, u32[]{:S(2)}) %copy-start.3) | copy-done | bytes 262168
  5.4 51.1 %shard_map.68 = (f32[8,2,128,128]{3,2,1,0:T(8,128)S(1)}, bf16[8,128,128]{2,1,0:T(8,128)(2,1)S(1)}) custom-call(s32[4,32]{1,0:T(4,128)S(1)} %copy-done.4, bf16[8,2,128,128]{3,2,1,0:T(8,128)(2,1)S(1)} %bitcast.7, bf16[8,2,128,128]{3,2,1,0:T(8,128)(2,1)S(1)} %bitcast.8, f32[8,128,128]{2,1,0:T(8,128)S(1)} %bitcast.9, bf16[8,128,128]{2,1,0:T(8,128)(2,1)S(1)} %bitcast.11), custom_call_target="tpu_custom_call" | custom-call | tf_op jit(solution)/shard_map/pallas_call | solution.py:669
  56.5 1.0 %copy.9 = f32[1,8,2,128,128]{4,3,2,1,0:T(8,128)} copy(f32[1,8,2,128,128]{4,3,2,1,0:T(8,128)S(1)} %bitcast.6) | data formatting | bytes 2097152
  57.5 0.7 %copy.10 = bf16[1,8,128,128]{3,2,1,0:T(8,128)(2,1)} copy(bf16[1,8,128,128]{3,2,1,0:T(8,128)(2,1)S(1)} %bitcast.10) | data formatting | bytes 524288
Async XLA Ops:
  0.6 0.7 %copy-start.4 = (s32[4,32]{1,0:T(4,128)S(1)}, s32[4,32]{1,0:T(4,128)}, u32[]{:S(2)}) copy-start(s32[4,32]{1,0:T(4,128)} %rows_ref.1) | copy-start | bytes 1540
  1.3 1.0 %copy-start = (bf16[1,8,2,128,128]{4,3,2,1,0:T(8,128)(2,1)S(1)}, bf16[1,8,2,128,128]{4,3,2,1,0:T(8,128)(2,1)}, u32[]{:S(2)}) copy-start(bf16[1,8,2,128,128]{4,3,2,1,0:T(8,128)(2,1)} %param.5) | copy-start | bytes 1572868
  2.4 1.0 %copy-start.1 = (bf16[1,8,2,128,128]{4,3,2,1,0:T(8,128)(2,1)S(1)}, bf16[1,8,2,128,128]{4,3,2,1,0:T(8,128)(2,1)}, u32[]{:S(2)}) copy-start(bf16[1,8,2,128,128]{4,3,2,1,0:T(8,128)(2,1)} %param.6) | copy-start | bytes 1572868
  3.4 1.0 %copy-start.2 = (f32[1,8,128,128]{3,2,1,0:T(8,128)S(1)}, f32[1,8,128,128]{3,2,1,0:T(8,128)}, u32[]{:S(2)}) copy-start(f32[1,8,128,128]{3,2,1,0:T(8,128)} %param.7) | copy-start | bytes 1572868
  4.4 0.9 %copy-start.3 = (bf16[1,8,128,128]{3,2,1,0:T(8,128)(2,1)S(1)}, bf16[1,8,128,128]{3,2,1,0:T(8,128)(2,1)}, u32[]{:S(2)}) copy-start(bf16[1,8,128,128]{3,2,1,0:T(8,128)(2,1)} %param.8) | copy-start | bytes 786436

commit v3 on v2

--- a/solution.py
+++ b/solution.py
@@ -36,24 +36,24 @@
     3: {3: (0, 128)},
 }
 SMOOTH_ROWS = {
-    1: {1: (152, 512), 2: (56, 152), 3: (0, 56)},
-    2: {2: (120, 256), 3: (0, 120)},
+    1: {1: (136, 512), 2: (56, 136), 3: (0, 56)},
+    2: {2: (64, 256), 3: (0, 64)},
     3: {3: (0, 128)},
 }
 SENT_UP = {
     0: {1: (72, 256), 2: (24, 72), 3: (0, 24)},
-    1: {2: (56, 128), 3: (0, 56)},
+    1: {2: (40, 128), 3: (0, 40)},
     2: {3: (0, 64)},
 }
 ORDER = {
-    0: (("down", 0), ("down", 1), ("down", 2), ("down", 3)),
-    1: (("down", 1), ("down", 2), ("down", 3), ("up", 1), ("up", 2), ("up", 3)),
-    2: (("down", 2), ("down", 3), ("up", 2), ("up", 3)),
-    3: (("down", 3), ("up", 3)),
+    0: "down0 down1 send1 down2 send2 down3 send3",
+    1: "down1 down2 down3 up2 up3 send3 send2 up1",
+    2: "down2 down3 up3 up2",
+    3: "down3 up3",
 }
 
 
-def over(first_col, col_count, rows, most, body):
+def over(col_at, col_count, rows, most, body):
     low, high = rows
     pieces = -(-(high - low) // most)
     size = -(-(high - low) // (8 * pieces)) * 8
@@ -62,7 +62,7 @@
         col = index // pieces
         part = index - col * pieces
         start = low if pieces == 1 else jnp.minimum(low + part * size, high - size)
-        body(first_col + col, start, size)
+        body(col_at + col if isinstance(col_at, int) else col_at(col), start, size)
         return carry
 
     lax.fori_loop(0, col_count * pieces, step, 0)
@@ -72,12 +72,16 @@
     levels,
     patches,
     rows_ref,
+    forcing_hbm,
+    velocity_hbm,
+    viscosity_hbm,
+    friction_hbm,
+    out_ref,
+    grad_ref,
     forcing,
     velocity,
     viscosity,
     friction,
-    out_ref,
-    grad_ref,
     mu,
     fric,
     mu_e,
@@ -113,6 +117,7 @@
     down_edge_recv,
     up_edge_send,
     up_edge_recv,
+    load_sem,
     init_sem,
     down_sem,
     down_edge_sem,
@@ -140,11 +145,25 @@
     fine_west = jnp.where(has_west, rows_ref[finer, west], 0)
     fine_east = jnp.where(has_east, rows_ref[finer, east], 0)
 
+    loads = [
+        pltpu.make_async_copy(src, dst, load_sem.at[i])
+        for i, (src, dst) in enumerate(
+            (
+                (viscosity_hbm, viscosity),
+                (friction_hbm, friction),
+                (forcing_hbm, forcing),
+                (velocity_hbm, velocity),
+            )
+        )
+    ]
+    for load in loads:
+        load.start()
+
     barrier = pltpu.get_barrier_semaphore()
     count = jnp.int32(0)
     for dl in (-1, 0, 1):
         for dp in (-1, 0, 1):
-            if dl == 0 and dp == 0:
+            if (dl == 0) == (dp == 0):
                 continue
             there = (level + dl >= 0) & (level + dl < levels) & (patch + dp >= 0) & (patch + dp < patches)
             count = count + jnp.where(there, 1, 0)
@@ -177,6 +196,9 @@
         return carry
 
     lax.fori_loop(0, cols + 2, clear, 0)
+
+    for load in loads[:3]:
+        load.wait()
 
     def unpack(slot_id, carry):
         col = slot_id // prows
@@ -225,56 +247,30 @@
             device_id_type=MESH,
         )
 
-    init_west = copy_to(
-        init_send.at[0], init_recv.at[0], init_sem.at[0], init_sem.at[2], level, -1
-    )
-    init_east = copy_to(
-        init_send.at[1], init_recv.at[1], init_sem.at[1], init_sem.at[3], level, 1
-    )
-
-    @pl.when(has_west)
-    def _():
-        init_west.start()
-
-    @pl.when(has_east)
-    def _():
-        init_east.start()
-
-    @pl.when(has_east)
-    def _():
-        init_west.wait_recv()
-
-    @pl.when(jnp.logical_not(has_east))
-    def _():
-        init_recv[0] = jnp.ones((SLOTS, 8, SIDE), F32)
-
-    @pl.when(has_west)
-    def _():
-        init_east.wait_recv()
-
-    @pl.when(jnp.logical_not(has_west))
-    def _():
-        init_recv[1] = jnp.ones((SLOTS, 8, SIDE), F32)
+    def init_copies(lv, side):
+        used = pl.ds(0, SLOTS // 2**lv)
+        return copy_to(
+            init_send.at[side, used],
+            init_recv.at[side, used],
+            init_sem.at[side],
+            init_sem.at[2 + side],
+            lv,
+            -1 if side == 0 else 1,
+        )
+
+    def init_each(act, flip):
+        for lv in range(levels):
+            for side in range(2):
+                there = has_west if (side == 0) != flip else has_east
+
+                @pl.when((level == lv) & there)
+                def _(lv=lv, side=side):
+                    act(init_copies(lv, side))
+
+    init_each(lambda copy: copy.start(), False)
 
     def spread(tile_t, index, first=0, count=SIDE):
         return jnp.broadcast_to(tile_t[first : first + count, index : index + 1], (count, SIDE))
-
-    def unpack_halo(row, carry):
-        for side in range(2):
-            col = cols + 1 if side == 0 else 0
-            base = base_of(jnp.int32(0) + col, row)
-            near = 0 if side == 0 else SIDE - 1
-            live = alive(row, east_rows if side == 0 else west_rows)
-            tile_t = jnp.transpose(init_recv[side, row])
-            mu[pl.ds(base, SIDE), :] = (
-                jnp.where(lane == near, spread(tile_t, 0), spread(tile_t, 1)) * live
-            )
-            fric[pl.ds(base, SIDE), :] = spread(tile_t, 2)
-            b_u[pl.ds(base, SIDE), :] = spread(tile_t, 3) * live
-            b_v[pl.ds(base, SIDE), :] = spread(tile_t, 4) * live
-        return carry
-
-    lax.fori_loop(0, prows, unpack_halo, 0)
 
     def coefficients(index, carry):
         col = index // prows
@@ -300,10 +296,6 @@
         half_v[pl.ds(base, SIDE), :] = live / d_v
         return carry
 
-    first = jnp.where(level == 0, prows, 0)
-    last = jnp.where(level == 0, 2 * prows, (cols + 2) * prows)
-    lax.fori_loop(first, last, coefficients, 0)
-
     quarter = SIDE // 2
     lane_row = lax.broadcasted_iota(jnp.int32, (SIDE, SIDE), 0)
     joins = [
@@ -315,7 +307,7 @@
         for half in range(2)
     ]
 
-    def program(lv):
+    def program(lv, early):
         columns = 2**lv
         tall = SLOTS // columns * SIDE
         step_col = tall + 2 * PAD
@@ -328,7 +320,7 @@
             rows = lax.broadcasted_iota(jnp.int32, (size, SIDE), 0) + start
             return rows < limit
 
-        def shift(src_u, src_v, rows):
+        def shift(src_u, src_v, rows, first=1, count=columns):
             def body(col, start, size):
                 base = at_row(col, start)
                 to_east = pl.multiple_of(base + step_col, 8)
@@ -343,7 +335,7 @@
                         jnp.where(here_lane == SIDE - 1, src[pl.ds(to_west, size), :], here), 1, 1
                     )
 
-            over(1, columns, rows, SIDE, body)
+            over(first, count, rows, SIDE, body)
 
         def residual_at(src_u, src_v, base, size):
             def at(ref, step=0):
@@ -373,11 +365,11 @@
         def sides():
             return ((0, has_west, has_east, -1), (1, has_east, has_west, 1))
 
-        def down_copies(sender, tier):
+        def down_copies(sender, tier, which=None):
             low, high = RESIDUAL_ROWS[sender][tier]
             low, high = low // 2, high // 2
             copies = []
-            for k in range(2**sender // 2):
+            for k in range(2**sender // 2) if which is None else which:
                 part = (slice(None), k, pl.ds(low, high - low))
                 copies.append(
                     copy_to(
@@ -431,8 +423,10 @@
                 dp,
             )
 
-        def start_edges(make, sender, tier):
+        def start_edges(make, sender, tier, which=(0, 1)):
             for side, there, _, dp in sides():
+                if side not in which:
+                    continue
                 copy = make(sender, tier, side, dp)
 
                 @pl.when(there)
@@ -441,18 +435,20 @@
 
                 pending.append((copy, there))
 
-        def wait_edges(make, sender, tier):
+        def wait_edges(make, sender, tier, which=(0, 1)):
             for side, _, there, dp in sides():
+                if side not in which:
+                    continue
                 copy = make(sender, tier, side, dp)
 
                 @pl.when(there)
                 def _(copy=copy):
                     copy.wait_recv()
 
-        def send_up(tier):
+        def fill_up_edges(tier, which=(0, 1)):
             low, high = SENT_UP[lv][tier]
             sources = (x_u, x_v) if lv == 0 else (y_u, y_v)
-            for side in range(2):
+            for side in which:
                 col = 1 if side == 0 else columns
                 near = 0 if side == 0 else SIDE - 1
                 parts = []
@@ -465,21 +461,23 @@
                             parts.append(jnp.zeros((1, SIDE), F32))
                 parts.append(jnp.zeros((4, SIDE), F32))
                 up_edge_send[tier, side] = jnp.concatenate(parts, axis=0)
+
+        def send_up(tier):
+            fill_up_edges(tier)
             start_edges(up_edge, lv, tier)
             for copy in up_copies(lv, tier):
                 copy.start()
                 pending.append((copy, None))
 
+        def start_body(col, start, size):
+            where = pl.ds(at_row(col, start), size)
+            x_u[where, :] = half_u[where, :] * b_u[where, :]
+            x_v[where, :] = half_v[where, :] * b_v[where, :]
+
         def down(tier):
             rows = START_ROWS[lv][tier]
             low, high = rows
             if tier == lv:
-
-                def start_body(col, start, size):
-                    where = pl.ds(at_row(col, start), size)
-                    x_u[where, :] = half_u[where, :] * b_u[where, :]
-                    x_v[where, :] = half_v[where, :] * b_v[where, :]
-
                 if lv == 0:
                     over(1, 1, rows, SIDE, start_body)
                 else:
@@ -514,23 +512,21 @@
 
                 over(1, columns, rows, SIDE, place_body)
             if lv == 0:
-                if tier > 0:
-                    send_up(tier)
                 return
             shift(x_u, x_v, rows)
-
-            def residual_body(col, start, size):
-                base = at_row(col, start)
-                _, _, r_u, r_v = residual_at(x_u, x_v, base, size)
-                y_u[pl.ds(base, size), :] = r_u
-                y_v[pl.ds(base, size), :] = r_v
-
             over(1, columns, RESIDUAL_ROWS[lv][tier], 64, residual_body)
+            send_down(tier, range(columns // 2))
+
+        def residual_body(col, start, size):
+            base = at_row(col, start)
+            _, _, r_u, r_v = residual_at(x_u, x_v, base, size)
+            y_u[pl.ds(base, size), :] = r_u
+            y_v[pl.ds(base, size), :] = r_v
+
+        def send_down(tier, which):
             low, high = RESIDUAL_ROWS[lv][tier]
             low, high = low // 2, high // 2
             pairs = columns // 2
-            copies = down_copies(lv, tier)
-
             def join_pair(k):
                 def join_body(_, start, size):
                     for comp, ref in enumerate((y_u, y_v)):
@@ -546,12 +542,14 @@
                         down_send[lv][comp, k, pl.ds(start, size), :] = total
 
                 over(0, 1, (low, high), 64, join_body)
-                copies[k].start()
-                pending.append((copies[k], None))
+                copy = down_copies(lv, tier, (k,))[0]
+                copy.start()
+                pending.append((copy, None))
 
             for k in sorted({0, pairs - 1}):
-                join_pair(k)
-            if lv > 1:
+                if k in which:
+                    join_pair(k)
+            if lv > 1 and 0 in which:
                 for side in range(2):
                     k = 0 if side == 0 else pairs - 1
                     near = 0 if side == 0 else SIDE - 1
@@ -567,12 +565,79 @@
                     down_edge_send[tier, side] = jnp.concatenate(parts, axis=0)
                 start_edges(down_edge, lv, tier)
             for k in range(1, pairs - 1):
-                join_pair(k)
+                if k in which:
+                    join_pair(k)
 
         def up(tier):
             low, high = SENT_UP[lv - 1][tier]
-            wait_edges(up_edge, lv - 1, tier)
-            for side in range(2):
+            halo_up(tier)
+            for copy in up_copies(lv - 1, tier):
+                copy.wait_recv()
+            prolong(tier, 0, columns // 2)
+            shift(z_u, z_v, (2 * low, 2 * high))
+            rows = SMOOTH_ROWS[lv][tier]
+            if lv == 2 and tier == 3:
+                copies = up_copies(lv, tier)
+                for col in range(1, columns + 1):
+                    over(col, 1, rows, 64, smooth_body)
+                    for copy in copies[2 * col - 2 : 2 * col]:
+                        copy.start()
+                        pending.append((copy, None))
+                    if col in (1, columns):
+                        side = 0 if col == 1 else 1
+                        fill_up_edges(tier, (side,))
+                        start_edges(up_edge, lv, tier, (side,))
+            else:
+                over(1, columns, rows, 64, smooth_body)
+
+        def smooth_body(col, start, size):
+            base = at_row(col, start)
+            where = pl.ds(base, size)
+            u, v, r_u, r_v = residual_at(z_u, z_v, base, size)
+            u = u + half_u[where, :] * r_u
+            v = v + half_v[where, :] * r_v
+            if lv < levels - 1:
+                y_u[where, :] = u
+                y_v[where, :] = v
+                return
+            slot = col - 1
+            lines = pl.ds(start, size)
+            live = alive(0, own_rows)
+            out_ref[slot, 0, lines, :] = u
+            out_ref[slot, 1, lines, :] = v
+            product = (
+                velocity[slot, 0, lines, :].astype(F32) * u
+                + velocity[slot, 1, lines, :].astype(F32) * v
+            )
+            grad_ref[slot, lines, :] = (
+                -(friction[slot, lines, :].astype(F32) * product) * live
+            ).astype(BF16)
+
+        def up_last():
+            tier = levels - 1
+            rows = (0, tall)
+            copies = up_copies(lv - 1, tier)
+            for k in range(4):
+                if k == 2:
+                    halo_up(tier, (1,))
+                if k == 3:
+                    halo_up(tier, (0,))
+                for copy in copies[2 * k : 2 * k + 2]:
+                    copy.wait_recv()
+                prolong(tier, k, 1)
+                if k > 0:
+                    first = 2 * k
+                    count = 3 if k == 3 else 2
+                    if k == 2:
+                        columns_at = lambda i: jnp.where(i == 0, 1, i + 3)
+                        first, count = columns_at, 3
+                    shift(z_u, z_v, rows, first, count)
+                    over(first, count, rows, 64, smooth_body)
+
+        def halo_up(tier, which=(0, 1)):
+            low, high = SENT_UP[lv - 1][tier]
+            wait_edges(up_edge, lv - 1, tier, which)
+            for side in which:
                 col = columns + 1 if side == 0 else 0
                 limit = quarter * (east_rows if side == 0 else west_rows)
                 tile_t = jnp.transpose(up_edge_recv[tier, side])
@@ -588,8 +653,9 @@
                         for step in range(2):
                             where = pl.ds(at_row(col, 2 * first) + step, size, stride=2)
                             to[where, :] = ref[where, :] + wide
-            for copy in up_copies(lv - 1, tier):
-                copy.wait_recv()
+
+        def prolong(tier, first, count):
+            low, high = SENT_UP[lv - 1][tier]
 
             def prolong_body(k, start, size):
                 keep = below(start, size, quarter * own_rows)
@@ -603,22 +669,30 @@
                             where = pl.ds(base + step, size, stride=2)
                             to[where, :] = ref[where, :] + wide
 
-            over(0, columns // 2, (low, high), 64, prolong_body)
-            shift(z_u, z_v, (2 * low, 2 * high))
-
-            def smooth_body(col, start, size):
-                base = at_row(col, start)
-                where = pl.ds(base, size)
-                u, v, r_u, r_v = residual_at(z_u, z_v, base, size)
-                y_u[where, :] = u + half_u[where, :] * r_u
-                y_v[where, :] = v + half_v[where, :] * r_v
-
-            over(1, columns, SMOOTH_ROWS[lv][tier], 64, smooth_body)
-            if lv < levels - 1 and tier > lv:
-                send_up(tier)
-
-        for stage, tier in ORDER[lv]:
-            (down if stage == "down" else up)(tier)
+            over(first, count, (low, high), 64, prolong_body)
+
+        if lv == levels - 1:
+            if early:
+                lax.fori_loop(2, columns, coefficients, 0)
+                over(2, columns - 2, (0, tall), SIDE, start_body)
+                shift(x_u, x_v, (0, tall), 3, columns - 4)
+                over(3, columns - 4, (0, tall), 64, residual_body)
+                send_down(lv, (1, 2))
+                return
+            ends = lambda i: jnp.where(i < 2, i, i + 6)
+            inner = lambda i: jnp.where(i < 2, i + 1, i + 5)
+            lax.fori_loop(0, 4, lambda i, carry: coefficients(ends(i), carry), 0)
+            over(ends, 4, (0, tall), SIDE, start_body)
+            shift(x_u, x_v, (0, tall), inner, 4)
+            over(inner, 4, (0, tall), 64, residual_body)
+            send_down(lv, (0, 3))
+            pending.extend((copy, None) for copy in down_copies(lv, lv, (1, 2)))
+            loads[3].wait()
+            up_last()
+        else:
+            for word in ORDER[lv].split():
+                {"down": down, "up": up, "send": send_up}[word[:-1]](int(word[-1]))
+            loads[3].wait()
 
         finals = (x_u, x_v) if lv == 0 else (y_u, y_v)
 
@@ -634,7 +708,8 @@
             product = velocity[slot, 0].astype(F32) * u + velocity[slot, 1].astype(F32) * v
             grad_ref[slot] = (-(friction[slot].astype(F32) * product) * live).astype(BF16)
 
-        over(1, columns, (0, tall), SIDE, finish)
+        if lv < levels - 1:
+            over(1, columns, (0, tall), SIDE, finish)
         for copy, there in pending:
             if there is None:
                 copy.wait_send()
@@ -644,19 +719,50 @@
                 def _(copy=copy):
                     copy.wait_send()
 
+    @pl.when(level == levels - 1)
+    def _():
+        program(levels - 1, True)
+
+    @pl.when(jnp.logical_not(has_east))
+    def _():
+        init_recv[0] = jnp.ones((SLOTS, 8, SIDE), F32)
+
+    @pl.when(jnp.logical_not(has_west))
+    def _():
+        init_recv[1] = jnp.ones((SLOTS, 8, SIDE), F32)
+
+    init_each(lambda copy: copy.wait_recv(), True)
+
+    def unpack_halo(row, carry):
+        for side in range(2):
+            col = cols + 1 if side == 0 else 0
+            base = base_of(jnp.int32(0) + col, row)
+            near = 0 if side == 0 else SIDE - 1
+            live = alive(row, east_rows if side == 0 else west_rows)
+            tile_t = jnp.transpose(init_recv[side, row])
+            mu[pl.ds(base, SIDE), :] = (
+                jnp.where(lane == near, spread(tile_t, 0), spread(tile_t, 1)) * live
+            )
+            fric[pl.ds(base, SIDE), :] = spread(tile_t, 2)
+            b_u[pl.ds(base, SIDE), :] = spread(tile_t, 3) * live
+            b_v[pl.ds(base, SIDE), :] = spread(tile_t, 4) * live
+        return carry
+
+    lax.fori_loop(0, prows, unpack_halo, 0)
+
+    @pl.when(level < levels - 1)
+    def _():
+        first = jnp.where(level == 0, prows, 0)
+        last = jnp.where(level == 0, 2 * prows, (cols + 2) * prows)
+        lax.fori_loop(first, last, coefficients, 0)
+
     for lv in range(levels):
 
         @pl.when(level == lv)
         def _(lv=lv):
-            program(lv)
-
-    @pl.when(has_west)
-    def _():
-        init_west.wait_send()
-
-    @pl.when(has_east)
-    def _():
-        init_east.wait_send()
+            program(lv, False)
+
+    init_each(lambda copy: copy.wait_send(), False)
 
 
 def per_device(levels, patches, forcing, velocity, viscosity, friction, patch_rows):
@@ -672,9 +778,16 @@
             jax.ShapeDtypeStruct((SLOTS, 2, SIDE, SIDE), F32),
             jax.ShapeDtypeStruct((SLOTS, SIDE, SIDE), BF16),
         ),
-        in_specs=[pl.BlockSpec(memory_space=pltpu.SMEM)] + [vmem] * 4,
+        in_specs=[pl.BlockSpec(memory_space=pltpu.SMEM)]
+        + [pl.BlockSpec(memory_space=pltpu.HBM)] * 4,
         out_specs=(vmem, vmem),
-        scratch_shapes=[tall] * 20
+        scratch_shapes=[
+            pltpu.VMEM((SLOTS, 2, SIDE, SIDE), BF16),
+            pltpu.VMEM((SLOTS, 2, SIDE, SIDE), BF16),
+            pltpu.VMEM((SLOTS, SIDE, SIDE), F32),
+            pltpu.VMEM((SLOTS, SIDE, SIDE), BF16),
+        ]
+        + [tall] * 20
         + [
             pltpu.VMEM((2, SLOTS, 8, SIDE), F32),
             pltpu.VMEM((2, SLOTS, 8, SIDE), F32),
@@ -682,6 +795,7 @@
         + [coarse[sender] for sender in range(1, levels)] * 3
         + [pltpu.VMEM((4, 2, 8, SIDE), F32)] * 4
         + [
+            pltpu.SemaphoreType.DMA((4,)),
             pltpu.SemaphoreType.DMA((4,)),
             pltpu.SemaphoreType.DMA((2, 16)),
             pltpu.SemaphoreType.DMA((2, 8)),
@@ -691,7 +805,13 @@
         compiler_params=pltpu.CompilerParams(
             collective_id=0, has_side_effects=True, vmem_limit_bytes=44 << 20
         ),
-    )(patch_rows, forcing[0], velocity[0], viscosity[0], friction[0])
+    )(
+        patch_rows,
+        *(
+            pltpu.with_memory_space_constraint(x[0], pltpu.HBM)
+            for x in (forcing, velocity, viscosity, friction)
+        ),
+    )
     return adjoint[None], gradient[None]
 
 

time: 58.5 us -> 50 us (0.85)
  Pallas kernels: 51.1 us -> 46.8 us
  local copies, waits for them, and re-layouts: 6.42 us -> 2.35 us
    pallas_call x1, Pallas kernels: 51.1 us -> 46.8 us  [per_device(): pl.pallas_call(functools.partial(kernel, levels, patches), out_shape=(jax...]
    unnamed x12 -> x4, local copies, waits for them, and re-layouts: 6.42 us -> 2.35 us
where the time goes in v3:
time: 50 us; the launch traced here: 49.8 us
  Pallas kernels  46.8 us (94%)
  local copies, waits for them, and re-layouts  2.35 us (5%)
  between operations  0.65 us (1%)
    pallas_call x1, Pallas kernels, per_device(): pl.pallas_call(functools.partial(kernel, levels, patches), out_shape=(jax...  46.8 us
    unnamed x4, local copies, waits for them, and re-layouts  2.35 us

profile of v3, /device:TPU:30, one launch (start us, length us, event | category | flops | bytes accessed | tf_op | source)
XLA Modules:
  0.0 49.8 jit_solution(15315571871151009308)
XLA Ops:
  0.6 0.0 copy-start
  0.6 0.7 %copy-done = s32[4,32]{1,0:T(4,128)S(1)} copy-done((s32[4,32]{1,0:T(4,128)S(1)}, s32[4,32]{1,0:T(4,128)}, u32[]{:S(2)}) %copy-start) | copy-done | bytes 536
  1.3 46.8 %shard_map.68 = (f32[8,2,128,128]{3,2,1,0:T(8,128)S(1)}, bf16[8,128,128]{2,1,0:T(8,128)(2,1)S(1)}) custom-call(s32[4,32]{1,0:T(4,128)S(1)} %copy-done, bf16[8,2,128,128]{3,2,1,0:T(8,128)(2,1)} %bitcast.8, bf16[8,2,128,128]{3,2,1,0:T(8,128)(2,1)} %bitcast.9, f32[8,128,128]{2,1,0:T(8,128)} %bitcast.10, bf16[8,128,128]{2,1,0:T(8,128)(2,1)} %bitcast.11), custom_call_target="tpu_custom_call" | custom-call | tf_op jit(solution)/shard_map/pallas_call | solution.py:775
  48.1 1.0 %copy.9 = f32[1,8,2,128,128]{4,3,2,1,0:T(8,128)} copy(f32[1,8,2,128,128]{4,3,2,1,0:T(8,128)S(1)} %bitcast.6) | data formatting | bytes 2097152
  49.1 0.7 %copy.10 = bf16[1,8,128,128]{3,2,1,0:T(8,128)(2,1)} copy(bf16[1,8,128,128]{3,2,1,0:T(8,128)(2,1)S(1)} %bitcast.7) | data formatting | bytes 524288
Async XLA Ops:
  0.6 0.7 %copy-start = (s32[4,32]{1,0:T(4,128)S(1)}, s32[4,32]{1,0:T(4,128)}, u32[]{:S(2)}) copy-start(s32[4,32]{1,0:T(4,128)} %rows_ref.1) | copy-start | bytes 1540

commit v4 on v3

--- a/solution.py
+++ b/solution.py
@@ -46,10 +46,9 @@
     2: {3: (0, 64)},
 }
 ORDER = {
-    0: "down0 down1 send1 down2 send2 down3 send3",
-    1: "down1 down2 down3 up2 up3 send3 send2 up1",
-    2: "down2 down3 up3 up2",
-    3: "down3 up3",
+    0: ("down0", "down1", "send1", "down2", "send2", "down3", "send3"),
+    1: ("down1", "down2", "down3", "up2", "up3", "send3", "send2", "up1"),
+    2: ("down2", "down3", "up3", "up2"),
 }
 
 
@@ -71,13 +70,14 @@
 def kernel(
     levels,
     patches,
-    rows_ref,
+    rows_hbm,
     forcing_hbm,
     velocity_hbm,
     viscosity_hbm,
     friction_hbm,
     out_ref,
     grad_ref,
+    rows_ref,
     forcing,
     velocity,
     viscosity,
@@ -117,12 +117,18 @@
     down_edge_recv,
     up_edge_send,
     up_edge_recv,
+    side_edge_send,
+    side_edge_recv,
+    base_edge_send,
+    base_edge_recv,
     load_sem,
     init_sem,
     down_sem,
     down_edge_sem,
     up_sem,
     up_edge_sem,
+    side_edge_sem,
+    base_edge_sem,
 ):
     down_send = {1: down_send_1, 2: down_send_2, 3: down_send_3}
     down_recv = {0: down_recv_0, 1: down_recv_1, 2: down_recv_2}
@@ -138,13 +144,6 @@
     finer = jnp.minimum(level + 1, levels - 1)
     west = jnp.maximum(patch - 1, 0)
     east = jnp.minimum(patch + 1, patches - 1)
-    own_rows = rows_ref[level, patch]
-    west_rows = jnp.where(has_west, rows_ref[level, west], 0)
-    east_rows = jnp.where(has_east, rows_ref[level, east], 0)
-    fine_own = rows_ref[finer, patch]
-    fine_west = jnp.where(has_west, rows_ref[finer, west], 0)
-    fine_east = jnp.where(has_east, rows_ref[finer, east], 0)
-
     loads = [
         pltpu.make_async_copy(src, dst, load_sem.at[i])
         for i, (src, dst) in enumerate(
@@ -153,6 +152,7 @@
                 (friction_hbm, friction),
                 (forcing_hbm, forcing),
                 (velocity_hbm, velocity),
+                (rows_hbm, rows_ref),
             )
         )
     ]
@@ -196,6 +196,14 @@
         return carry
 
     lax.fori_loop(0, cols + 2, clear, 0)
+
+    loads[4].wait()
+    own_rows = rows_ref[level, patch]
+    west_rows = jnp.where(has_west, rows_ref[level, west], 0)
+    east_rows = jnp.where(has_east, rows_ref[level, east], 0)
+    fine_own = rows_ref[finer, patch]
+    fine_west = jnp.where(has_west, rows_ref[finer, west], 0)
+    fine_east = jnp.where(has_east, rows_ref[finer, east], 0)
 
     for load in loads[:3]:
         load.wait()
@@ -423,6 +431,36 @@
                 dp,
             )
 
+        def side_edge(sender, tier, side, dp):
+            return copy_to(
+                side_edge_send.at[tier, side],
+                side_edge_recv.at[tier, side],
+                side_edge_sem.at[0, tier * 2 + side],
+                side_edge_sem.at[1, tier * 2 + side],
+                1,
+                dp,
+            )
+
+        def base_edge(sender, tier, side, dp):
+            return copy_to(
+                base_edge_send.at[side],
+                base_edge_recv.at[side],
+                base_edge_sem.at[side],
+                base_edge_sem.at[2 + side],
+                1,
+                dp,
+            )
+
+        def edges_of(refs, low, high):
+            blocks = []
+            for ref in refs:
+                for part in range(2):
+                    if part * SIDE < high and low < (part + 1) * SIDE:
+                        blocks.append(jnp.transpose(ref(part * SIDE)))
+            return [
+                [block[near : near + 1] for block in blocks] for near in (0, SIDE - 1)
+            ]
+
         def start_edges(make, sender, tier, which=(0, 1)):
             for side, there, _, dp in sides():
                 if side not in which:
@@ -463,8 +501,9 @@
                 up_edge_send[tier, side] = jnp.concatenate(parts, axis=0)
 
         def send_up(tier):
-            fill_up_edges(tier)
-            start_edges(up_edge, lv, tier)
+            if lv > 0:
+                fill_up_edges(tier)
+                start_edges(up_edge, lv, tier)
             for copy in up_copies(lv, tier):
                 copy.start()
                 pending.append((copy, None))
@@ -483,7 +522,7 @@
                 else:
                     over(0, columns + 2, rows, SIDE, start_body)
             else:
-                if lv > 0:
+                def halos():
                     wait_edges(down_edge, lv + 1, tier)
                     for side in range(2):
                         col = columns + 1 if side == 0 else 0
@@ -496,6 +535,9 @@
                         ):
                             got = spread(tile_t, comp, low, high - low)
                             to[where, :] = half[where, :] * jnp.where(keep, got, ref[where, :])
+
+                if lv == 2:
+                    halos()
                 for copy in down_copies(lv + 1, tier):
                     copy.wait_recv()
 
@@ -511,6 +553,8 @@
                         to[where, :] = half[where, :] * new
 
                 over(1, columns, rows, SIDE, place_body)
+                if lv == 1:
+                    halos()
             if lv == 0:
                 return
             shift(x_u, x_v, rows)
@@ -542,13 +586,27 @@
                         down_send[lv][comp, k, pl.ds(start, size), :] = total
 
                 over(0, 1, (low, high), 64, join_body)
-                copy = down_copies(lv, tier, (k,))[0]
-                copy.start()
-                pending.append((copy, None))
-
-            for k in sorted({0, pairs - 1}):
-                if k in which:
-                    join_pair(k)
+            def start_pairs(ks):
+                for copy in down_copies(lv, tier, ks):
+                    copy.start()
+                    pending.append((copy, None))
+
+            outer = tuple(k for k in sorted({0, pairs - 1}) if k in which)
+            for k in outer:
+                join_pair(k)
+            if lv == 1:
+                start_pairs(outer)
+                refs = [
+                    lambda row, comp=comp: down_send[1][comp, 0, pl.ds(row, SIDE), :]
+                    for comp in range(2)
+                ]
+                for side, lines in enumerate(edges_of(refs, low, high)):
+                    if len(lines) == 2:
+                        blank = jnp.zeros((1, SIDE), F32)
+                        lines = [lines[0], blank, lines[1], blank]
+                    lines = lines + [jnp.zeros((4, SIDE), F32)]
+                    side_edge_send[tier, side] = jnp.concatenate(lines, axis=0)
+                start_edges(side_edge, lv, tier)
             if lv > 1 and 0 in which:
                 for side in range(2):
                     k = 0 if side == 0 else pairs - 1
@@ -564,29 +622,37 @@
                     parts.append(jnp.zeros((6, SIDE), F32))
                     down_edge_send[tier, side] = jnp.concatenate(parts, axis=0)
                 start_edges(down_edge, lv, tier)
+            if lv > 1:
+                start_pairs(outer)
             for k in range(1, pairs - 1):
                 if k in which:
                     join_pair(k)
+                    start_pairs((k,))
 
         def up(tier):
             low, high = SENT_UP[lv - 1][tier]
-            halo_up(tier)
+            if lv == 1:
+                halo_up(tier)
             for copy in up_copies(lv - 1, tier):
                 copy.wait_recv()
             prolong(tier, 0, columns // 2)
+            if lv > 1:
+                halo_up(tier)
             shift(z_u, z_v, (2 * low, 2 * high))
             rows = SMOOTH_ROWS[lv][tier]
             if lv == 2 and tier == 3:
                 copies = up_copies(lv, tier)
-                for col in range(1, columns + 1):
+                for col in (1, 4, 2, 3):
                     over(col, 1, rows, 64, smooth_body)
+                    if col == 4:
+                        fill_up_edges(tier)
+                        start_edges(up_edge, lv, tier)
+                        continue
                     for copy in copies[2 * col - 2 : 2 * col]:
                         copy.start()
-                        pending.append((copy, None))
-                    if col in (1, columns):
-                        side = 0 if col == 1 else 1
-                        fill_up_edges(tier, (side,))
-                        start_edges(up_edge, lv, tier, (side,))
+                for copy in copies[6:8]:
+                    copy.start()
+                pending.extend((copy, None) for copy in copies)
             else:
                 over(1, columns, rows, 64, smooth_body)
 
@@ -617,30 +683,35 @@
             tier = levels - 1
             rows = (0, tall)
             copies = up_copies(lv - 1, tier)
+            def columns_done(first, count):
+                shift(z_u, z_v, rows, first, count)
+                over(first, count, rows, 64, smooth_body)
+
             for k in range(4):
-                if k == 2:
-                    halo_up(tier, (1,))
-                if k == 3:
-                    halo_up(tier, (0,))
                 for copy in copies[2 * k : 2 * k + 2]:
                     copy.wait_recv()
                 prolong(tier, k, 1)
-                if k > 0:
-                    first = 2 * k
-                    count = 3 if k == 3 else 2
-                    if k == 2:
-                        columns_at = lambda i: jnp.where(i == 0, 1, i + 3)
-                        first, count = columns_at, 3
-                    shift(z_u, z_v, rows, first, count)
-                    over(first, count, rows, 64, smooth_body)
+                if k in (1, 2):
+                    columns_done(2 * k, 2)
+                if k == 2:
+                    halo_up(tier)
+                    columns_done(1, 1)
+            columns_done(6, 3)
 
         def halo_up(tier, which=(0, 1)):
             low, high = SENT_UP[lv - 1][tier]
-            wait_edges(up_edge, lv - 1, tier, which)
+            wait_edges(side_edge if lv == 1 else up_edge, lv - 1, tier, which)
             for side in which:
                 col = columns + 1 if side == 0 else 0
                 limit = quarter * (east_rows if side == 0 else west_rows)
-                tile_t = jnp.transpose(up_edge_recv[tier, side])
+                tile = (side_edge_recv if lv == 1 else up_edge_recv)[tier, side]
+                if lv == 1:
+                    spot = lax.broadcasted_iota(jnp.int32, (8, SIDE), 0) % 2 * SIDE + lane[:8]
+                    known = base_edge_recv[side]
+                    factor = jnp.concatenate([known[:4], known[:4]], axis=0)
+                    plain = jnp.concatenate([known[4:], known[4:]], axis=0)
+                    tile = factor * jnp.where(spot < limit, tile, plain)
+                tile_t = jnp.transpose(tile)
                 for part in range(2):
                     first, last = max(low, part * SIDE), min(high, (part + 1) * SIDE)
                     if first >= last:
@@ -673,24 +744,35 @@
 
         if lv == levels - 1:
             if early:
-                lax.fori_loop(2, columns, coefficients, 0)
-                over(2, columns - 2, (0, tall), SIDE, start_body)
-                shift(x_u, x_v, (0, tall), 3, columns - 4)
+                lax.fori_loop(1, columns + 1, coefficients, 0)
+                over(1, columns, (0, tall), SIDE, start_body)
+                shift(x_u, x_v, (0, tall), 2, columns - 2)
                 over(3, columns - 4, (0, tall), 64, residual_body)
                 send_down(lv, (1, 2))
+                over(lambda i: 2 + 5 * i, 2, (0, tall), 64, residual_body)
                 return
             ends = lambda i: jnp.where(i < 2, i, i + 6)
-            inner = lambda i: jnp.where(i < 2, i + 1, i + 5)
+            inner = lambda i: 1 + 7 * i
             lax.fori_loop(0, 4, lambda i, carry: coefficients(ends(i), carry), 0)
             over(ends, 4, (0, tall), SIDE, start_body)
-            shift(x_u, x_v, (0, tall), inner, 4)
-            over(inner, 4, (0, tall), 64, residual_body)
+            shift(x_u, x_v, (0, tall), inner, 2)
+            over(inner, 2, (0, tall), 64, residual_body)
             send_down(lv, (0, 3))
             pending.extend((copy, None) for copy in down_copies(lv, lv, (1, 2)))
             loads[3].wait()
             up_last()
         else:
-            for word in ORDER[lv].split():
+            if lv == 0:
+                refs = [
+                    lambda row, ref=ref: ref[pl.ds(at_row(1, row), SIDE), :]
+                    for ref in (half_u, half_v, b_u, b_v)
+                ]
+                for side, lines in enumerate(edges_of(refs, 0, 2 * SIDE)):
+                    base_edge_send[side] = jnp.concatenate(lines, axis=0)
+                start_edges(base_edge, lv, 0)
+            for word in ORDER[lv]:
+                if lv == 1 and word == "up2":
+                    wait_edges(base_edge, 0, 0)
                 {"down": down, "up": up, "send": send_up}[word[:-1]](int(word[-1]))
             loads[3].wait()
 
@@ -763,6 +845,17 @@
             program(lv, False)
 
     init_each(lambda copy: copy.wait_send(), False)
+
+
+def write_out(adjoint, gradient, adjoint_hbm, gradient_hbm, sem):
+    copies = [
+        pltpu.make_async_copy(adjoint, adjoint_hbm, sem.at[0]),
+        pltpu.make_async_copy(gradient, gradient_hbm, sem.at[1]),
+    ]
+    for copy in copies:
+        copy.start()
+    for copy in copies:
+        copy.wait()
 
 
 def per_device(levels, patches, forcing, velocity, viscosity, friction, patch_rows):
@@ -778,10 +871,10 @@
             jax.ShapeDtypeStruct((SLOTS, 2, SIDE, SIDE), F32),
             jax.ShapeDtypeStruct((SLOTS, SIDE, SIDE), BF16),
         ),
-        in_specs=[pl.BlockSpec(memory_space=pltpu.SMEM)]
-        + [pl.BlockSpec(memory_space=pltpu.HBM)] * 4,
+        in_specs=[pl.BlockSpec(memory_space=pltpu.HBM)] * 5,
         out_specs=(vmem, vmem),
         scratch_shapes=[
+            pltpu.SMEM((levels, patches), jnp.int32),
             pltpu.VMEM((SLOTS, 2, SIDE, SIDE), BF16),
             pltpu.VMEM((SLOTS, 2, SIDE, SIDE), BF16),
             pltpu.VMEM((SLOTS, SIDE, SIDE), F32),
@@ -793,25 +886,38 @@
             pltpu.VMEM((2, SLOTS, 8, SIDE), F32),
         ]
         + [coarse[sender] for sender in range(1, levels)] * 3
-        + [pltpu.VMEM((4, 2, 8, SIDE), F32)] * 4
+        + [pltpu.VMEM((4, 2, 8, SIDE), F32)] * 6
+        + [pltpu.VMEM((2, 8, SIDE), F32)] * 2
         + [
-            pltpu.SemaphoreType.DMA((4,)),
+            pltpu.SemaphoreType.DMA((5,)),
             pltpu.SemaphoreType.DMA((4,)),
             pltpu.SemaphoreType.DMA((2, 16)),
             pltpu.SemaphoreType.DMA((2, 8)),
             pltpu.SemaphoreType.DMA((2, 32)),
             pltpu.SemaphoreType.DMA((2, 8)),
+            pltpu.SemaphoreType.DMA((2, 8)),
+            pltpu.SemaphoreType.DMA((4,)),
         ],
         compiler_params=pltpu.CompilerParams(
             collective_id=0, has_side_effects=True, vmem_limit_bytes=44 << 20
         ),
     )(
-        patch_rows,
         *(
-            pltpu.with_memory_space_constraint(x[0], pltpu.HBM)
-            for x in (forcing, velocity, viscosity, friction)
+            pltpu.with_memory_space_constraint(x, pltpu.HBM)
+            for x in (patch_rows, forcing[0], velocity[0], viscosity[0], friction[0])
+        )
+    )
+    adjoint, gradient = pl.pallas_call(
+        write_out,
+        out_shape=(
+            jax.ShapeDtypeStruct(adjoint.shape, adjoint.dtype),
+            jax.ShapeDtypeStruct(gradient.shape, gradient.dtype),
         ),
-    )
+        in_specs=[vmem, vmem],
+        out_specs=(pl.BlockSpec(memory_space=pltpu.HBM),) * 2,
+        scratch_shapes=[pltpu.SemaphoreType.DMA((2,))],
+        compiler_params=pltpu.CompilerParams(vmem_limit_bytes=4 << 20),
+    )(adjoint, gradient)
     return adjoint[None], gradient[None]
 
 

time: 50 us -> 43.6 us (0.87)
  Pallas kernels: 46.8 us -> 42.9 us
  local copies, waits for them, and re-layouts: 2.35 us -> 0 us
    pallas_call x1, Pallas kernels: 46.8 us -> 41.8 us  [per_device(): pl.pallas_call(functools.partial(kernel, levels, patches), out_shape=(jax...]
    unnamed x4 -> x0, local copies, waits for them, and re-layouts: 2.35 us -> none
    pallas_call x0 -> x1, Pallas kernels: none -> 1.07 us  [per_device(): pl.pallas_call(write_out, out_shape=(jax.ShapeDtypeStruct(adjoint.shape,...]
where the time goes in v4:
time: 43.6 us; the launch traced here: 43.5 us
  Pallas kernels  42.9 us (98%)
  between operations  0.64 us (1%)
    pallas_call x1, Pallas kernels, per_device(): pl.pallas_call(functools.partial(kernel, levels, patches), out_shape=(jax...  41.8 us
    pallas_call x1, Pallas kernels, per_device(): pl.pallas_call(write_out, out_shape=(jax.ShapeDtypeStruct(adjoint.shape,...  1.07 us

profile of v4, /device:TPU:30, one launch (start us, length us, event | category | flops | bytes accessed | tf_op | source)
XLA Modules:
  0.0 43.5 jit_solution(7534496572072961614)
XLA Ops:
  0.6 41.8 %shard_map.68 = (f32[8,2,128,128]{3,2,1,0:T(8,128)S(1)}, bf16[8,128,128]{2,1,0:T(8,128)(2,1)S(1)}) custom-call(s32[4,32]{1,0:T(4,128)} %rows_hbm.1, bf16[8,2,128,128]{3,2,1,0:T(8,128)(2,1)} %bitcast.6, bf16[8,2,128,128]{3,2,1,0:T(8,128)(2,1)} %bitcast.7, f32[8,128,128]{2,1,0:T(8,128)} %bitcast.8, bf16[8,128,128]{2,1,0:T(8,128)(2,1)} %bitcast.9), custom_call_target="tpu_custom_call" | custom-call | tf_op jit(solution)/shard_map/pallas_call | solution.py:868
  42.4 1.1 %shard_map.69 = (f32[8,2,128,128]{3,2,1,0:T(8,128)}, bf16[8,128,128]{2,1,0:T(8,128)(2,1)}) custom-call(f32[8,2,128,128]{3,2,1,0:T(8,128)S(1)} %get-tuple-element.6.adjoint, bf16[8,128,128]{2,1,0:T(8,128)(2,1)S(1)} %get-tuple-element.7.gradient), custom_call_target="tpu_custom_call" | custom-call | tf_op jit(solution)/shard_map/pallas_call | solution.py:910

commit v5 on v4

--- a/solution.py
+++ b/solution.py
@@ -46,8 +46,8 @@
     2: {3: (0, 64)},
 }
 ORDER = {
-    0: ("down0", "down1", "send1", "down2", "send2", "down3", "send3"),
-    1: ("down1", "down2", "down3", "up2", "up3", "send3", "send2", "up1"),
+    0: ("down0", "down1", "down2", "down3"),
+    1: ("down1", "known0", "down2", "down3", "up2", "up3", "send3", "send2", "up1"),
     2: ("down2", "down3", "up3", "up2"),
 }
 
@@ -117,8 +117,8 @@
     down_edge_recv,
     up_edge_send,
     up_edge_recv,
-    side_edge_send,
-    side_edge_recv,
+    halo_sum,
+    known_halo,
     base_edge_send,
     base_edge_recv,
     load_sem,
@@ -127,7 +127,6 @@
     down_edge_sem,
     up_sem,
     up_edge_sem,
-    side_edge_sem,
     base_edge_sem,
 ):
     down_send = {1: down_send_1, 2: down_send_2, 3: down_send_3}
@@ -225,17 +224,17 @@
     def pack(row, carry):
         for side in range(2):
             base = base_of(jnp.where(side == 0, 1, cols), row)
-            near, far = (0, 1) if side == 0 else (SIDE - 1, SIDE - 2)
+            four = slice(0, 4) if side == 0 else slice(SIDE - 4, SIDE)
+            three = slice(0, 3) if side == 0 else slice(SIDE - 3, SIDE)
             mu_t = jnp.transpose(mu[pl.ds(base, SIDE), :])
             fr_t = jnp.transpose(fric[pl.ds(base, SIDE), :])
             bu_t = jnp.transpose(b_u[pl.ds(base, SIDE), :])
             bv_t = jnp.transpose(b_v[pl.ds(base, SIDE), :])
             parts = [
-                mu_t[near : near + 1],
-                mu_t[far : far + 1],
-                fr_t[near : near + 1],
-                bu_t[near : near + 1],
-                bv_t[near : near + 1],
+                mu_t[four],
+                fr_t[three],
+                bu_t[three],
+                bv_t[three],
                 jnp.zeros((3, SIDE), F32),
             ]
             init_send[side, row] = jnp.concatenate(parts, axis=0)
@@ -276,6 +275,14 @@
                     act(init_copies(lv, side))
 
     init_each(lambda copy: copy.start(), False)
+
+    def columns_of(tile):
+        blank = jnp.zeros((SIDE - tile.shape[0], SIDE), F32)
+        return jnp.transpose(jnp.concatenate([tile, blank], axis=0))
+
+    def lanes_from(tile_t, side, first, width):
+        steps = (-first if side == 0 else SIDE - width - first) % SIDE
+        return tile_t if steps == 0 else pltpu.roll(tile_t, steps, 1)
 
     def spread(tile_t, index, first=0, count=SIDE):
         return jnp.broadcast_to(tile_t[first : first + count, index : index + 1], (count, SIDE))
@@ -331,8 +338,8 @@
         def shift(src_u, src_v, rows, first=1, count=columns):
             def body(col, start, size):
                 base = at_row(col, start)
-                to_east = pl.multiple_of(base + step_col, 8)
-                to_west = pl.multiple_of(base - step_col, 8)
+                to_east = pl.multiple_of(base + jnp.where(col == columns + 1, 0, step_col), 8)
+                to_west = pl.multiple_of(base - jnp.where(col == 0, 0, step_col), 8)
                 here_lane = lane[:size]
                 for src, dst_e, dst_w in ((src_u, ue, uw), (src_v, ve, vw)):
                     here = src[pl.ds(base, size), :]
@@ -431,15 +438,31 @@
                 dp,
             )
 
-        def side_edge(sender, tier, side, dp):
-            return copy_to(
-                side_edge_send.at[tier, side],
-                side_edge_recv.at[tier, side],
-                side_edge_sem.at[0, tier * 2 + side],
-                side_edge_sem.at[1, tier * 2 + side],
-                1,
-                dp,
-            )
+        def known_copies():
+            rows = 2 * SIDE
+            return [
+                copy_to(
+                    ref.at[pl.ds(SLOTS * SIDE + 2 * PAD + PAD, rows)],
+                    up_recv[1].at[comp, 0, pl.ds(0, rows)],
+                    up_sem.at[0, comp],
+                    up_sem.at[1, comp],
+                    1,
+                    0,
+                )
+                for comp, ref in enumerate((half_u, half_v))
+            ]
+
+        def known():
+            wait_edges(base_edge, 0, 0)
+            tiles = [jnp.transpose(base_edge_recv[side]) for side in range(2)]
+            for comp in range(2):
+                for part in range(2):
+                    index = 2 * comp + part
+                    known_halo[comp, pl.ds(part * SIDE, SIDE), :] = jnp.where(
+                        lane < quarter, spread(tiles[0], index), spread(tiles[1], index)
+                    )
+            for copy in known_copies():
+                copy.wait_recv()
 
         def base_edge(sender, tier, side, dp):
             return copy_to(
@@ -456,7 +479,8 @@
             for ref in refs:
                 for part in range(2):
                     if part * SIDE < high and low < (part + 1) * SIDE:
-                        blocks.append(jnp.transpose(ref(part * SIDE)))
+                        rows = pl.ds(at_row(1, part * SIDE), SIDE)
+                        blocks.append(jnp.transpose(ref[rows, :]))
             return [
                 [block[near : near + 1] for block in blocks] for near in (0, SIDE - 1)
             ]
@@ -501,9 +525,8 @@
                 up_edge_send[tier, side] = jnp.concatenate(parts, axis=0)
 
         def send_up(tier):
-            if lv > 0:
-                fill_up_edges(tier)
-                start_edges(up_edge, lv, tier)
+            fill_up_edges(tier)
+            start_edges(up_edge, lv, tier)
             for copy in up_copies(lv, tier):
                 copy.start()
                 pending.append((copy, None))
@@ -527,14 +550,16 @@
                     for side in range(2):
                         col = columns + 1 if side == 0 else 0
                         limit = quarter * (fine_east if side == 0 else fine_west)
-                        tile_t = jnp.transpose(down_edge_recv[tier, side])
+                        tile_t = columns_of(down_edge_recv[tier, side])[low:high]
                         where = pl.ds(at_row(col, low), high - low)
                         keep = below(low, high - low, limit)
                         for comp, (ref, half, to) in enumerate(
                             ((b_u, half_u, x_u), (b_v, half_v, x_v))
                         ):
-                            got = spread(tile_t, comp, low, high - low)
-                            to[where, :] = half[where, :] * jnp.where(keep, got, ref[where, :])
+                            got = lanes_from(tile_t, side, 3 * comp, 3)
+                            new = jnp.where(keep, got, ref[where, :])
+                            ref[where, :] = new
+                            to[where, :] = half[where, :] * new
 
                 if lv == 2:
                     halos()
@@ -557,8 +582,9 @@
                     halos()
             if lv == 0:
                 return
-            shift(x_u, x_v, rows)
-            over(1, columns, RESIDUAL_ROWS[lv][tier], 64, residual_body)
+            first, count = (0, columns + 2) if lv == 1 else (1, columns)
+            shift(x_u, x_v, rows, first, count)
+            over(first, count, RESIDUAL_ROWS[lv][tier], 64, residual_body)
             send_down(tier, range(columns // 2))
 
         def residual_body(col, start, size):
@@ -571,19 +597,25 @@
             low, high = RESIDUAL_ROWS[lv][tier]
             low, high = low // 2, high // 2
             pairs = columns // 2
-            def join_pair(k):
+            def join_halo(low, high):
+                join_pair(0, (columns + 1, 0), halo_sum)
+
+            def join_pair(k, pair=None, to=None):
+                pair = (2 * k + 1, 2 * k + 2) if pair is None else pair
+                to = down_send[lv].at[:, k] if to is None else to
+
                 def join_body(_, start, size):
                     for comp, ref in enumerate((y_u, y_v)):
                         total = None
                         for half in range(2):
-                            base = at_row(2 * k + half + 1, 2 * start)
+                            base = at_row(pair[half], 2 * start)
                             lines = (
                                 ref[pl.ds(base, size, stride=2), :]
                                 + ref[pl.ds(base + 1, size, stride=2), :]
                             )
                             term = split_dot(lines, joins[half])
                             total = term if total is None else total + term
-                        down_send[lv][comp, k, pl.ds(start, size), :] = total
+                        to[comp, pl.ds(start, size), :] = total
 
                 over(0, 1, (low, high), 64, join_body)
             def start_pairs(ks):
@@ -596,30 +628,20 @@
                 join_pair(k)
             if lv == 1:
                 start_pairs(outer)
-                refs = [
-                    lambda row, comp=comp: down_send[1][comp, 0, pl.ds(row, SIDE), :]
-                    for comp in range(2)
-                ]
-                for side, lines in enumerate(edges_of(refs, low, high)):
-                    if len(lines) == 2:
-                        blank = jnp.zeros((1, SIDE), F32)
-                        lines = [lines[0], blank, lines[1], blank]
-                    lines = lines + [jnp.zeros((4, SIDE), F32)]
-                    side_edge_send[tier, side] = jnp.concatenate(lines, axis=0)
-                start_edges(side_edge, lv, tier)
+                join_halo(low, high)
             if lv > 1 and 0 in which:
                 for side in range(2):
                     k = 0 if side == 0 else pairs - 1
-                    near = 0 if side == 0 else SIDE - 1
+                    three = slice(0, 3) if side == 0 else slice(SIDE - 3, SIDE)
                     lines = min(SIDE, tall // 2)
                     parts = []
                     for comp in range(2):
                         block_t = jnp.transpose(down_send[lv][comp, k, pl.ds(0, lines), :])
-                        line = block_t[near : near + 1]
+                        line = block_t[three]
                         if lines < SIDE:
                             line = jnp.concatenate([line, line], axis=1)
                         parts.append(line)
-                    parts.append(jnp.zeros((6, SIDE), F32))
+                    parts.append(jnp.zeros((2, SIDE), F32))
                     down_edge_send[tier, side] = jnp.concatenate(parts, axis=0)
                 start_edges(down_edge, lv, tier)
             if lv > 1:
@@ -633,8 +655,9 @@
             low, high = SENT_UP[lv - 1][tier]
             if lv == 1:
                 halo_up(tier)
-            for copy in up_copies(lv - 1, tier):
-                copy.wait_recv()
+            if lv > 1:
+                for copy in up_copies(lv - 1, tier):
+                    copy.wait_recv()
             prolong(tier, 0, columns // 2)
             if lv > 1:
                 halo_up(tier)
@@ -700,18 +723,26 @@
 
         def halo_up(tier, which=(0, 1)):
             low, high = SENT_UP[lv - 1][tier]
-            wait_edges(side_edge if lv == 1 else up_edge, lv - 1, tier, which)
+            if lv == 1:
+                def halo_body(_, start, size):
+                    limit = quarter * jnp.where(lane[:size] < quarter, east_rows, west_rows)
+                    keep = lax.broadcasted_iota(jnp.int32, (size, SIDE), 0) + start < limit
+                    for comp, (ref, to) in enumerate(((x_u, z_u), (x_v, z_v))):
+                        lines = pl.ds(start, size)
+                        wide = known_halo[comp, lines, :] * halo_sum[comp, lines, :]
+                        wide = jnp.where(keep, wide, 0.0)
+                        for col in (0, columns + 1):
+                            for step in range(2):
+                                where = pl.ds(at_row(col, 2 * start) + step, size, stride=2)
+                                to[where, :] = ref[where, :] + wide
+
+                over(0, 1, (low, high), 64, halo_body)
+                return
+            wait_edges(up_edge, lv - 1, tier, which)
             for side in which:
                 col = columns + 1 if side == 0 else 0
                 limit = quarter * (east_rows if side == 0 else west_rows)
-                tile = (side_edge_recv if lv == 1 else up_edge_recv)[tier, side]
-                if lv == 1:
-                    spot = lax.broadcasted_iota(jnp.int32, (8, SIDE), 0) % 2 * SIDE + lane[:8]
-                    known = base_edge_recv[side]
-                    factor = jnp.concatenate([known[:4], known[:4]], axis=0)
-                    plain = jnp.concatenate([known[4:], known[4:]], axis=0)
-                    tile = factor * jnp.where(spot < limit, tile, plain)
-                tile_t = jnp.transpose(tile)
+                tile_t = jnp.transpose(up_edge_recv[tier, side])
                 for part in range(2):
                     first, last = max(low, part * SIDE), min(high, (part + 1) * SIDE)
                     if first >= last:
@@ -732,6 +763,8 @@
                 keep = below(start, size, quarter * own_rows)
                 for comp, (ref, to) in enumerate(((x_u, z_u), (x_v, z_v))):
                     coarse = up_recv[lv][comp, k, pl.ds(start, size), :]
+                    if lv == 1:
+                        coarse = coarse * down_send[1][comp, k, pl.ds(start, size), :]
                     coarse = jnp.where(keep, coarse, 0.0)
                     for half in range(2):
                         base = at_row(2 * k + half + 1, 2 * start)
@@ -763,16 +796,17 @@
             up_last()
         else:
             if lv == 0:
-                refs = [
-                    lambda row, ref=ref: ref[pl.ds(at_row(1, row), SIDE), :]
-                    for ref in (half_u, half_v, b_u, b_v)
-                ]
-                for side, lines in enumerate(edges_of(refs, 0, 2 * SIDE)):
+                for copy in known_copies():
+                    copy.start()
+                    pending.append((copy, None))
+                for side, lines in enumerate(edges_of((half_u, half_v), 0, 2 * SIDE)):
+                    lines.append(jnp.zeros((4, SIDE), F32))
                     base_edge_send[side] = jnp.concatenate(lines, axis=0)
                 start_edges(base_edge, lv, 0)
             for word in ORDER[lv]:
-                if lv == 1 and word == "up2":
-                    wait_edges(base_edge, 0, 0)
+                if word == "known0":
+                    known()
+                    continue
                 {"down": down, "up": up, "send": send_up}[word[:-1]](int(word[-1]))
             loads[3].wait()
 
@@ -807,11 +841,11 @@
 
     @pl.when(jnp.logical_not(has_east))
     def _():
-        init_recv[0] = jnp.ones((SLOTS, 8, SIDE), F32)
+        init_recv[0] = jnp.ones((SLOTS, 16, SIDE), F32)
 
     @pl.when(jnp.logical_not(has_west))
     def _():
-        init_recv[1] = jnp.ones((SLOTS, 8, SIDE), F32)
+        init_recv[1] = jnp.ones((SLOTS, 16, SIDE), F32)
 
     init_each(lambda copy: copy.wait_recv(), True)
 
@@ -819,15 +853,17 @@
         for side in range(2):
             col = cols + 1 if side == 0 else 0
             base = base_of(jnp.int32(0) + col, row)
-            near = 0 if side == 0 else SIDE - 1
             live = alive(row, east_rows if side == 0 else west_rows)
-            tile_t = jnp.transpose(init_recv[side, row])
-            mu[pl.ds(base, SIDE), :] = (
-                jnp.where(lane == near, spread(tile_t, 0), spread(tile_t, 1)) * live
-            )
-            fric[pl.ds(base, SIDE), :] = spread(tile_t, 2)
-            b_u[pl.ds(base, SIDE), :] = spread(tile_t, 3) * live
-            b_v[pl.ds(base, SIDE), :] = spread(tile_t, 4) * live
+            tile_t = columns_of(init_recv[side, row])
+
+            def place(first, width, other):
+                valid = lane < width if side == 0 else lane >= SIDE - width
+                return jnp.where(valid, lanes_from(tile_t, side, first, width), other)
+
+            mu[pl.ds(base, SIDE), :] = place(0, 4, 0.0) * live
+            fric[pl.ds(base, SIDE), :] = place(4, 3, 1.0)
+            b_u[pl.ds(base, SIDE), :] = place(7, 3, 0.0) * live
+            b_v[pl.ds(base, SIDE), :] = place(10, 3, 0.0) * live
         return carry
 
     lax.fori_loop(0, prows, unpack_halo, 0)
@@ -882,11 +918,12 @@
         ]
         + [tall] * 20
         + [
-            pltpu.VMEM((2, SLOTS, 8, SIDE), F32),
-            pltpu.VMEM((2, SLOTS, 8, SIDE), F32),
+            pltpu.VMEM((2, SLOTS, 16, SIDE), F32),
+            pltpu.VMEM((2, SLOTS, 16, SIDE), F32),
         ]
         + [coarse[sender] for sender in range(1, levels)] * 3
-        + [pltpu.VMEM((4, 2, 8, SIDE), F32)] * 6
+        + [pltpu.VMEM((4, 2, 8, SIDE), F32)] * 4
+        + [pltpu.VMEM((2, 2 * SIDE, SIDE), F32)] * 2
         + [pltpu.VMEM((2, 8, SIDE), F32)] * 2
         + [
             pltpu.SemaphoreType.DMA((5,)),
@@ -894,7 +931,6 @@
             pltpu.SemaphoreType.DMA((2, 16)),
             pltpu.SemaphoreType.DMA((2, 8)),
             pltpu.SemaphoreType.DMA((2, 32)),
-            pltpu.SemaphoreType.DMA((2, 8)),
             pltpu.SemaphoreType.DMA((2, 8)),
             pltpu.SemaphoreType.DMA((4,)),
         ],

time: 43.6 us -> 40.5 us (0.929)
  Pallas kernels: 42.9 us -> 39.7 us
    pallas_call x1, Pallas kernels: 41.8 us -> 38.7 us  [per_device(): pl.pallas_call(functools.partial(kernel, levels, patches), out_shape=(jax...]
where the time goes in v5:
time: 40.5 us; the launch traced here: 40.4 us
  Pallas kernels  39.7 us (98%)
  between operations  0.64 us (2%)
    pallas_call x1, Pallas kernels, per_device(): pl.pallas_call(functools.partial(kernel, levels, patches), out_shape=(jax...  38.7 us
    pallas_call x1, Pallas kernels, per_device(): pl.pallas_call(write_out, out_shape=(jax.ShapeDtypeStruct(adjoint.shape,...  1.07 us

profile of v5, /device:TPU:30, one launch (start us, length us, event | category | flops | bytes accessed | tf_op | source)
XLA Modules:
  0.0 40.4 jit_solution(1668518037547017218)
XLA Ops:
  0.6 38.7 %shard_map.68 = (f32[8,2,128,128]{3,2,1,0:T(8,128)S(1)}, bf16[8,128,128]{2,1,0:T(8,128)(2,1)S(1)}) custom-call(s32[4,32]{1,0:T(4,128)} %rows_hbm.1, bf16[8,2,128,128]{3,2,1,0:T(8,128)(2,1)} %bitcast.6, bf16[8,2,128,128]{3,2,1,0:T(8,128)(2,1)} %bitcast.7, f32[8,128,128]{2,1,0:T(8,128)} %bitcast.8, bf16[8,128,128]{2,1,0:T(8,128)(2,1)} %bitcast.9), custom_call_target="tpu_custom_call" | custom-call | tf_op jit(solution)/shard_map/pallas_call | solution.py:904
  39.3 1.1 %shard_map.69 = (f32[8,2,128,128]{3,2,1,0:T(8,128)}, bf16[8,128,128]{2,1,0:T(8,128)(2,1)}) custom-call(f32[8,2,128,128]{3,2,1,0:T(8,128)S(1)} %get-tuple-element.6.adjoint, bf16[8,128,128]{2,1,0:T(8,128)(2,1)S(1)} %get-tuple-element.7.gradient), custom_call_target="tpu_custom_call" | custom-call | tf_op jit(solution)/shard_map/pallas_call | solution.py:946

commit v6 on v5

--- a/solution.py
+++ b/solution.py
@@ -52,19 +52,33 @@
 }
 
 
-def over(col_at, col_count, rows, most, body):
+def over(col_at, col_count, rows, most, body, group=1):
     low, high = rows
     pieces = -(-(high - low) // most)
     size = -(-(high - low) // (8 * pieces)) * 8
-
-    def step(index, carry):
-        col = index // pieces
-        part = index - col * pieces
-        start = low if pieces == 1 else jnp.minimum(low + part * size, high - size)
+    total = col_count * pieces
+
+    def step(index):
+        if isinstance(index, int):
+            col, part = divmod(index, pieces)
+            start = min(low + part * size, high - size)
+        else:
+            col = index // pieces
+            part = index - col * pieces
+            start = low if pieces == 1 else jnp.minimum(low + part * size, high - size)
         body(col_at + col if isinstance(col_at, int) else col_at(col), start, size)
+
+    def steps(index, carry):
+        for inner in range(group):
+            step(index * group + inner)
         return carry
 
-    lax.fori_loop(0, col_count * pieces, step, 0)
+    done = 0
+    if total > group:
+        lax.fori_loop(0, total // group, steps, 0)
+        done = total // group * group
+    for index in range(done, total):
+        step(index)
 
 
 def kernel(
@@ -242,7 +256,6 @@
 
     lax.fori_loop(0, prows, pack, 0)
 
-    pl.semaphore_wait(barrier, count)
 
     def copy_to(src, dst, send, recv, there, dp):
         return pltpu.make_async_remote_copy(
@@ -274,7 +287,6 @@
                 def _(lv=lv, side=side):
                     act(init_copies(lv, side))
 
-    init_each(lambda copy: copy.start(), False)
 
     def columns_of(tile):
         blank = jnp.zeros((SIDE - tile.shape[0], SIDE), F32)
@@ -350,7 +362,7 @@
                         jnp.where(here_lane == SIDE - 1, src[pl.ds(to_west, size), :], here), 1, 1
                     )
 
-            over(first, count, rows, SIDE, body)
+            over(first, count, rows, SIDE, body, 4 if rows[1] - rows[0] <= 80 else 2)
 
         def residual_at(src_u, src_v, base, size):
             def at(ref, step=0):
@@ -577,14 +589,14 @@
                         ref[where, :] = new
                         to[where, :] = half[where, :] * new
 
-                over(1, columns, rows, SIDE, place_body)
+                over(1, columns, rows, SIDE, place_body, 4 if rows[1] <= 64 else 1)
                 if lv == 1:
                     halos()
             if lv == 0:
                 return
             first, count = (0, columns + 2) if lv == 1 else (1, columns)
             shift(x_u, x_v, rows, first, count)
-            over(first, count, RESIDUAL_ROWS[lv][tier], 64, residual_body)
+            over(first, count, RESIDUAL_ROWS[lv][tier], 64, residual_body, 2)
             send_down(tier, range(columns // 2))
 
         def residual_body(col, start, size):
@@ -659,25 +671,32 @@
                 for copy in up_copies(lv - 1, tier):
                     copy.wait_recv()
             prolong(tier, 0, columns // 2)
+            rows = SMOOTH_ROWS[lv][tier]
+            fine = (2 * low, 2 * high)
+            if lv == 2 and tier == 3:
+                copies = up_copies(lv, tier)
+
+                def ready(col):
+                    for copy in copies[2 * col - 2 : 2 * col]:
+                        copy.start()
+
+                shift(z_u, z_v, fine, 2, 2)
+                for col in (2, 3):
+                    over(col, 1, rows, 64, smooth_body)
+                    ready(col)
+                halo_up(tier)
+                shift(z_u, z_v, fine, lambda i: 1 + 3 * i, 2)
+                over(lambda i: 1 + 3 * i, 2, rows, 64, smooth_body, 2)
+                fill_up_edges(tier)
+                start_edges(up_edge, lv, tier)
+                for col in (1, 4):
+                    ready(col)
+                pending.extend((copy, None) for copy in copies)
+                return
             if lv > 1:
                 halo_up(tier)
-            shift(z_u, z_v, (2 * low, 2 * high))
-            rows = SMOOTH_ROWS[lv][tier]
-            if lv == 2 and tier == 3:
-                copies = up_copies(lv, tier)
-                for col in (1, 4, 2, 3):
-                    over(col, 1, rows, 64, smooth_body)
-                    if col == 4:
-                        fill_up_edges(tier)
-                        start_edges(up_edge, lv, tier)
-                        continue
-                    for copy in copies[2 * col - 2 : 2 * col]:
-                        copy.start()
-                for copy in copies[6:8]:
-                    copy.start()
-                pending.extend((copy, None) for copy in copies)
-            else:
-                over(1, columns, rows, 64, smooth_body)
+            shift(z_u, z_v, fine)
+            over(1, columns, rows, 64, smooth_body, 2)
 
         def smooth_body(col, start, size):
             base = at_row(col, start)
@@ -708,15 +727,16 @@
             copies = up_copies(lv - 1, tier)
             def columns_done(first, count):
                 shift(z_u, z_v, rows, first, count)
-                over(first, count, rows, 64, smooth_body)
-
-            for k in range(4):
+                over(first, count, rows, 64, smooth_body, 2)
+
+            for k in (1, 2, 0, 3):
                 for copy in copies[2 * k : 2 * k + 2]:
                     copy.wait_recv()
                 prolong(tier, k, 1)
-                if k in (1, 2):
-                    columns_done(2 * k, 2)
                 if k == 2:
+                    columns_done(4, 2)
+                if k == 0:
+                    columns_done(2, 2)
                     halo_up(tier)
                     columns_done(1, 1)
             columns_done(6, 3)
@@ -773,23 +793,25 @@
                             where = pl.ds(base + step, size, stride=2)
                             to[where, :] = ref[where, :] + wide
 
-            over(first, count, (low, high), 64, prolong_body)
+            over(first, count, (low, high), 64, prolong_body, 2)
 
         if lv == levels - 1:
             if early:
-                lax.fori_loop(1, columns + 1, coefficients, 0)
-                over(1, columns, (0, tall), SIDE, start_body)
-                shift(x_u, x_v, (0, tall), 2, columns - 2)
-                over(3, columns - 4, (0, tall), 64, residual_body)
+                if early == 1:
+                    lax.fori_loop(1, columns + 1, coefficients, 0)
+                    over(1, columns, (0, tall), SIDE, start_body, 2)
+                    shift(x_u, x_v, (0, tall), 2, columns - 2)
+                    return
+                over(3, columns - 4, (0, tall), 64, residual_body, 2)
                 send_down(lv, (1, 2))
-                over(lambda i: 2 + 5 * i, 2, (0, tall), 64, residual_body)
+                over(lambda i: 2 + 5 * i, 2, (0, tall), 64, residual_body, 2)
                 return
             ends = lambda i: jnp.where(i < 2, i, i + 6)
             inner = lambda i: 1 + 7 * i
             lax.fori_loop(0, 4, lambda i, carry: coefficients(ends(i), carry), 0)
             over(ends, 4, (0, tall), SIDE, start_body)
             shift(x_u, x_v, (0, tall), inner, 2)
-            over(inner, 2, (0, tall), 64, residual_body)
+            over(inner, 2, (0, tall), 64, residual_body, 2)
             send_down(lv, (0, 3))
             pending.extend((copy, None) for copy in down_copies(lv, lv, (1, 2)))
             loads[3].wait()
@@ -837,7 +859,14 @@
 
     @pl.when(level == levels - 1)
     def _():
-        program(levels - 1, True)
+        program(levels - 1, 1)
+
+    pl.semaphore_wait(barrier, count)
+    init_each(lambda copy: copy.start(), False)
+
+    @pl.when(level == levels - 1)
+    def _():
+        program(levels - 1, 2)
 
     @pl.when(jnp.logical_not(has_east))
     def _():
@@ -878,7 +907,7 @@
 
         @pl.when(level == lv)
         def _(lv=lv):
-            program(lv, False)
+            program(lv, 0)
 
     init_each(lambda copy: copy.wait_send(), False)
 

time: 40.5 us -> 37.5 us (0.926)
  Pallas kernels: 39.7 us -> 36.7 us
    pallas_call x1, Pallas kernels: 38.7 us -> 35.6 us  [per_device(): pl.pallas_call(functools.partial(kernel, levels, patches), out_shape=(jax...]
where the time goes in v6:
time: 37.5 us; the launch traced here: 37.3 us
  Pallas kernels  36.7 us (98%)
  between operations  0.64 us (2%)
    pallas_call x1, Pallas kernels, per_device(): pl.pallas_call(functools.partial(kernel, levels, patches), out_shape=(jax...  35.6 us
    pallas_call x1, Pallas kernels, per_device(): pl.pallas_call(write_out, out_shape=(jax.ShapeDtypeStruct(adjoint.shape,...  1.07 us

profile of v6, /device:TPU:30, one launch (start us, length us, event | category | flops | bytes accessed | tf_op | source)
XLA Modules:
  0.0 37.3 jit_solution(12297768719957316464)
XLA Ops:
  0.6 35.6 %shard_map.68 = (f32[8,2,128,128]{3,2,1,0:T(8,128)S(1)}, bf16[8,128,128]{2,1,0:T(8,128)(2,1)S(1)}) custom-call(s32[4,32]{1,0:T(4,128)} %rows_hbm.1, bf16[8,2,128,128]{3,2,1,0:T(8,128)(2,1)} %bitcast.6, bf16[8,2,128,128]{3,2,1,0:T(8,128)(2,1)} %bitcast.7, f32[8,128,128]{2,1,0:T(8,128)} %bitcast.8, bf16[8,128,128]{2,1,0:T(8,128)(2,1)} %bitcast.9), custom_call_target="tpu_custom_call" | custom-call | tf_op jit(solution)/shard_map/pallas_call | solution.py:933
  36.2 1.1 %shard_map.69 = (f32[8,2,128,128]{3,2,1,0:T(8,128)}, bf16[8,128,128]{2,1,0:T(8,128)(2,1)}) custom-call(f32[8,2,128,128]{3,2,1,0:T(8,128)S(1)} %get-tuple-element.6.adjoint, bf16[8,128,128]{2,1,0:T(8,128)(2,1)S(1)} %get-tuple-element.7.gradient), custom_call_target="tpu_custom_call" | custom-call | tf_op jit(solution)/shard_map/pallas_call | solution.py:975

commit v7 on v6

--- a/solution.py
+++ b/solution.py
@@ -47,7 +47,7 @@
 }
 ORDER = {
     0: ("down0", "down1", "down2", "down3"),
-    1: ("down1", "known0", "down2", "down3", "up2", "up3", "send3", "send2", "up1"),
+    1: ("down1", "down2", "known0", "down3", "up2", "up3", "send3", "send2", "up1"),
     2: ("down2", "down3", "up3", "up2"),
 }
 
@@ -552,7 +552,17 @@
             rows = START_ROWS[lv][tier]
             low, high = rows
             if tier == lv:
-                if lv == 0:
+                if lv == 2:
+                    ends = lambda i: jnp.where(i < 2, i, i + 2)
+                    lax.fori_loop(
+                        0,
+                        8,
+                        lambda i, carry: coefficients(ends(i // 2) * 2 + i % 2, carry),
+                        0,
+                    )
+                    for col in (0, 1, 4, 5):
+                        over(col, 1, rows, SIDE, start_body, 2)
+                elif lv == 0:
                     over(1, 1, rows, SIDE, start_body)
                 else:
                     over(0, columns + 2, rows, SIDE, start_body)
@@ -595,6 +605,8 @@
             if lv == 0:
                 return
             first, count = (0, columns + 2) if lv == 1 else (1, columns)
+            if lv == tier == 2:
+                first, count = lambda i: 1 + 3 * i, 2
             shift(x_u, x_v, rows, first, count)
             over(first, count, RESIDUAL_ROWS[lv][tier], 64, residual_body, 2)
             send_down(tier, range(columns // 2))
@@ -795,6 +807,14 @@
 
             over(first, count, (low, high), 64, prolong_body, 2)
 
+        if lv == 2 and early:
+            if early == 1:
+                lax.fori_loop(2, 10, coefficients, 0)
+                over(1, columns, START_ROWS[2][2], SIDE, start_body, 2)
+                return
+            shift(x_u, x_v, START_ROWS[2][2], 2, 2)
+            over(2, 2, RESIDUAL_ROWS[2][2], 64, residual_body, 2)
+            return
         if lv == levels - 1:
             if early:
                 if early == 1:
@@ -857,16 +877,20 @@
                 def _(copy=copy):
                     copy.wait_send()
 
-    @pl.when(level == levels - 1)
-    def _():
-        program(levels - 1, 1)
+    for lv in (2, 3):
+
+        @pl.when(level == lv)
+        def _(lv=lv):
+            program(lv, 1)
 
     pl.semaphore_wait(barrier, count)
     init_each(lambda copy: copy.start(), False)
 
-    @pl.when(level == levels - 1)
-    def _():
-        program(levels - 1, 2)
+    for lv in (2, 3):
+
+        @pl.when(level == lv)
+        def _(lv=lv):
+            program(lv, 2)
 
     @pl.when(jnp.logical_not(has_east))
     def _():
@@ -897,7 +921,7 @@
 
     lax.fori_loop(0, prows, unpack_halo, 0)
 
-    @pl.when(level < levels - 1)
+    @pl.when(level < 2)
     def _():
         first = jnp.where(level == 0, prows, 0)
         last = jnp.where(level == 0, 2 * prows, (cols + 2) * prows)

time: 37.5 us -> 36.6 us (0.976)
  Pallas kernels: 36.7 us -> 35.8 us
    pallas_call x1, Pallas kernels: 35.6 us -> 34.8 us  [per_device(): pl.pallas_call(functools.partial(kernel, levels, patches), out_shape=(jax...]
where the time goes in v7:
time: 36.6 us; the launch traced here: 36.5 us
  Pallas kernels  35.8 us (98%)
  between operations  0.64 us (2%)
    pallas_call x1, Pallas kernels, per_device(): pl.pallas_call(functools.partial(kernel, levels, patches), out_shape=(jax...  34.8 us
    pallas_call x1, Pallas kernels, per_device(): pl.pallas_call(write_out, out_shape=(jax.ShapeDtypeStruct(adjoint.shape,...  1.07 us

profile of v7, /device:TPU:30, one launch (start us, length us, event | category | flops | bytes accessed | tf_op | source)
XLA Modules:
  0.0 36.5 jit_solution(5005046301156524114)
XLA Ops:
  0.6 34.8 %shard_map.68 = (f32[8,2,128,128]{3,2,1,0:T(8,128)S(1)}, bf16[8,128,128]{2,1,0:T(8,128)(2,1)S(1)}) custom-call(s32[4,32]{1,0:T(4,128)} %rows_hbm.1, bf16[8,2,128,128]{3,2,1,0:T(8,128)(2,1)} %bitcast.6, bf16[8,2,128,128]{3,2,1,0:T(8,128)(2,1)} %bitcast.7, f32[8,128,128]{2,1,0:T(8,128)} %bitcast.8, bf16[8,128,128]{2,1,0:T(8,128)(2,1)} %bitcast.9), custom_call_target="tpu_custom_call" | custom-call | tf_op jit(solution)/shard_map/pallas_call | solution.py:957
  35.4 1.1 %shard_map.69 = (f32[8,2,128,128]{3,2,1,0:T(8,128)}, bf16[8,128,128]{2,1,0:T(8,128)(2,1)}) custom-call(f32[8,2,128,128]{3,2,1,0:T(8,128)S(1)} %get-tuple-element.6.adjoint, bf16[8,128,128]{2,1,0:T(8,128)(2,1)S(1)} %get-tuple-element.7.gradient), custom_call_target="tpu_custom_call" | custom-call | tf_op jit(solution)/shard_map/pallas_call | solution.py:999

commit v8 on v7

--- a/solution.py
+++ b/solution.py
@@ -278,9 +278,9 @@
             -1 if side == 0 else 1,
         )
 
-    def init_each(act, flip):
-        for lv in range(levels):
-            for side in range(2):
+    def init_each(act, flip, which=range(levels), sides=(0, 1)):
+        for lv in which:
+            for side in sides:
                 there = has_west if (side == 0) != flip else has_east
 
                 @pl.when((level == lv) & there)
@@ -653,8 +653,9 @@
             if lv == 1:
                 start_pairs(outer)
                 join_halo(low, high)
-            if lv > 1 and 0 in which:
-                for side in range(2):
+            edge_sides = [side for side, k in ((0, 0), (1, pairs - 1)) if k in which]
+            if lv > 1 and edge_sides:
+                for side in edge_sides:
                     k = 0 if side == 0 else pairs - 1
                     three = slice(0, 3) if side == 0 else slice(SIDE - 3, SIDE)
                     lines = min(SIDE, tall // 2)
@@ -667,7 +668,7 @@
                         parts.append(line)
                     parts.append(jnp.zeros((2, SIDE), F32))
                     down_edge_send[tier, side] = jnp.concatenate(parts, axis=0)
-                start_edges(down_edge, lv, tier)
+                start_edges(down_edge, lv, tier, edge_sides)
             if lv > 1:
                 start_pairs(outer)
             for k in range(1, pairs - 1):
@@ -826,14 +827,29 @@
                 send_down(lv, (1, 2))
                 over(lambda i: 2 + 5 * i, 2, (0, tall), 64, residual_body, 2)
                 return
-            ends = lambda i: jnp.where(i < 2, i, i + 6)
-            inner = lambda i: 1 + 7 * i
-            lax.fori_loop(0, 4, lambda i, carry: coefficients(ends(i), carry), 0)
-            over(ends, 4, (0, tall), SIDE, start_body)
-            shift(x_u, x_v, (0, tall), inner, 2)
-            over(inner, 2, (0, tall), 64, residual_body, 2)
-            send_down(lv, (0, 3))
-            pending.extend((copy, None) for copy in down_copies(lv, lv, (1, 2)))
+
+            def end_of_row(side):
+                init_each(lambda copy: copy.wait_recv(), True, (lv,), (side,))
+                unpack_halo(0, 0, (side,))
+                own = columns if side == 0 else 1
+                for col in (own, columns + 1 if side == 0 else 0):
+                    coefficients(jnp.int32(col), 0)
+                over(min(own, own + 1 - 2 * side), 2, (0, tall), SIDE, start_body, 2)
+                shift(x_u, x_v, (0, tall), own, 1)
+                over(own, 1, (0, tall), 64, residual_body, 2)
+                send_down(lv, (3,) if side == 0 else (0,))
+
+            for parity in range(2):
+
+                @pl.when(patch % 2 == parity)
+                def _(parity=parity):
+                    for side in (parity, 1 - parity):
+                        end_of_row(side)
+
+            pending.clear()
+            pending.extend((copy, None) for copy in down_copies(lv, lv))
+            for side, there, _, dp in sides():
+                pending.append((down_edge(lv, lv, side, dp), there))
             loads[3].wait()
             up_last()
         else:
@@ -900,10 +916,10 @@
     def _():
         init_recv[1] = jnp.ones((SLOTS, 16, SIDE), F32)
 
-    init_each(lambda copy: copy.wait_recv(), True)
-
-    def unpack_halo(row, carry):
-        for side in range(2):
+    init_each(lambda copy: copy.wait_recv(), True, range(levels - 1))
+
+    def unpack_halo(row, carry, sides=(0, 1)):
+        for side in sides:
             col = cols + 1 if side == 0 else 0
             base = base_of(jnp.int32(0) + col, row)
             live = alive(row, east_rows if side == 0 else west_rows)
@@ -919,7 +935,9 @@
             b_v[pl.ds(base, SIDE), :] = place(10, 3, 0.0) * live
         return carry
 
-    lax.fori_loop(0, prows, unpack_halo, 0)
+    @pl.when(level < levels - 1)
+    def _():
+        lax.fori_loop(0, prows, unpack_halo, 0)
 
     @pl.when(level < 2)
     def _():

time: 36.6 us -> 36.1 us (0.986)
  Pallas kernels: 35.8 us -> 35.3 us
    pallas_call x1, Pallas kernels: 34.8 us -> 34.2 us  [per_device(): pl.pallas_call(functools.partial(kernel, levels, patches), out_shape=(jax...]
where the time goes in v8:
time: 36.1 us; the launch traced here: 35.9 us
  Pallas kernels  35.3 us (98%)
  between operations  0.64 us (2%)
    pallas_call x1, Pallas kernels, per_device(): pl.pallas_call(functools.partial(kernel, levels, patches), out_shape=(jax...  34.2 us
    pallas_call x1, Pallas kernels, per_device(): pl.pallas_call(write_out, out_shape=(jax.ShapeDtypeStruct(adjoint.shape,...  1.07 us

profile of v8, /device:TPU:30, one launch (start us, length us, event | category | flops | bytes accessed | tf_op | source)
XLA Modules:
  0.0 35.9 jit_solution(7048492309572061818)
XLA Ops:
  0.6 34.2 %shard_map.68 = (f32[8,2,128,128]{3,2,1,0:T(8,128)S(1)}, bf16[8,128,128]{2,1,0:T(8,128)(2,1)S(1)}) custom-call(s32[4,32]{1,0:T(4,128)} %rows_hbm.1, bf16[8,2,128,128]{3,2,1,0:T(8,128)(2,1)} %bitcast.6, bf16[8,2,128,128]{3,2,1,0:T(8,128)(2,1)} %bitcast.7, f32[8,128,128]{2,1,0:T(8,128)} %bitcast.8, bf16[8,128,128]{2,1,0:T(8,128)(2,1)} %bitcast.9), custom_call_target="tpu_custom_call" | custom-call | tf_op jit(solution)/shard_map/pallas_call | solution.py:975
  34.9 1.1 %shard_map.69 = (f32[8,2,128,128]{3,2,1,0:T(8,128)}, bf16[8,128,128]{2,1,0:T(8,128)(2,1)}) custom-call(f32[8,2,128,128]{3,2,1,0:T(8,128)S(1)} %get-tuple-element.6.adjoint, bf16[8,128,128]{2,1,0:T(8,128)(2,1)S(1)} %get-tuple-element.7.gradient), custom_call_target="tpu_custom_call" | custom-call | tf_op jit(solution)/shard_map/pallas_call | solution.py:1017
